TPU v7x, 128 devices: a whole 4x4x4 slice. The times are simulated.
128 devices in a mesh: comp: 4 (over x), tile: 32 (over y, z, core).
Axes of the slice: x: 4, y: 4, z: 4, core: 2. Of those that a mesh axis runs over, the one named last changes fastest.
Arguments:
- atmos_column_state: float32 [128, 524288], P(None, ('comp', 'tile')), may hold values from -6 to 6
- vertical_column_operator: float32 [128, 128], replicated, may hold values from -0.5 to 0.5
- level_flux_weight: float32 [128], replicated, may hold values from -0.5 to 0.5
- coupling_response: float32 [128], replicated, may hold values from -4 to 4
- remap_weight_blocks: bfloat16 [8, 128, 128], replicated, may hold values from -0.5 to 0.5
- remap_source_row: int32 [40960, 4], P('tile'), may hold values from 0 to 4095
- remap_entry_block: int32 [40960, 4], P('tile'), may hold values from 0 to 7
- remap_entry_present: int32 [40960, 4], P('tile'), may hold values from 0 to 1, as said below
- ocean_land_mask: int32 [2048, 2560], P('tile'), may hold values 0 or 1
- depth_diagonal_added: float32 [2048, 2560], P('tile'), may hold values from 0.001 to 0.1
- ocean_surface_temp: float32 [2048, 2560], P('tile'), may hold values from -6 to 6
- sea_temp_source_row: int32 [4096], P(('comp', 'tile')), may hold values from 0 to 40959
Outputs:
- atm_out: float32 [128, 524288], P(None, ('comp', 'tile'))
- surface_height: float32 [2048, 2560], P('tile')
Inputs may be any that keep to these rules, and one draw needn't show every extreme that they name: `remap_entry_present`: 1 where the entry counts, 0 where it doesn't.
All inputs are finite; a program needn't handle non-finite values. No bound on the sum of `ocean_land_mask` on one device may be relied on, other than what follows from the above.
Results may differ from a plain program's by a relative error of at most 0.0029.
Values may be sent and summed in bfloat16 or wider, within the bound.
A program may use at most 64 MiB of HBM per device.

v0:
```python
import functools

import jax
import jax.numpy as jnp
from jax import lax
from jax.experimental import pallas as pl
from jax.experimental.pallas import tpu as pltpu
from jax.sharding import PartitionSpec as P

F32, BF16, I32 = jnp.float32, jnp.bfloat16, jnp.int32
MESH = pl.DeviceIdType.MESH
LANES = 128
HALO = 8
TIME_STEP = 0.5


def kernel(
    groups,
    tiles,
    state_hbm,
    vco_ref,
    weight_ref,
    blocks_ref,
    source_ref,
    entry_ref,
    present_ref,
    mask_ref,
    depth_ref,
    temp_ref,
    wanted_ref,
    pre_hbm,
    height_hbm,
    rows_out,
    state,
    vv,
    fluxf,
    flux_all,
    table,
    idx_v,
    idx_s,
    coef,
    field,
    w0,
    w1,
    w2,
    height,
    req_v,
    picks,
    sst,
    rows_send,
    rows_recv,
    gram_send,
    gram_recv,
    in_sem,
    out_sem,
    idx_sem,
    height_sem,
    flux_ssem,
    flux_rsem,
    req_ssem,
    req_rsem,
    halo_ssem,
    halo_rsem,
    gram_ssem,
    gram_rsem,
    rows_ssem,
    rows_rsem,
):
    group, tile = lax.axis_index("comp"), lax.axis_index("tile")
    count = groups * tiles
    me = group * tiles + tile
    lev, cols = state.shape
    own = mask_ref.shape[0]
    width = mask_ref.shape[1]
    per = width // LANES
    ext = own + 2 * HALO
    nrows = cols // LANES
    n_flux = count * nrows
    n_ocean = source_ref.shape[1]
    n_block = blocks_ref.shape[0]
    chunk = min(1024, cols)
    n_chunk = cols // chunk

    def peer_of(i):
        other = lax.rem(me + i, count)
        return lax.div(other, tiles), lax.rem(other, tiles), other

    barrier = pltpu.get_barrier_semaphore()

    def greet(i, carry):
        g, t, _ = peer_of(i)
        pl.semaphore_signal(barrier, inc=1, device_id=(g, t), device_id_type=MESH)
        return carry

    lax.fori_loop(1, count, greet, 0)

    def load_state(i):
        part = pl.ds(i * chunk, chunk)
        return pltpu.make_async_copy(state_hbm.at[:, part], state.at[:, part], in_sem.at[i])

    for i in range(n_chunk):
        load_state(i).start()

    vco = vco_ref[...]
    v_hi = vco.astype(BF16)
    v_lo = (vco - v_hi.astype(F32)).astype(BF16)
    vv[0:lev, 0:lev] = v_hi
    vv[0:lev, lev : 2 * lev] = v_hi
    vv[lev : 2 * lev, 0:lev] = v_lo
    vv[lev : 2 * lev, lev : 2 * lev] = v_lo

    mask = mask_ref[...].astype(F32)
    coef[HALO : HALO + own, :] = mask * (4.0 + depth_ref[...])
    spare = n_block * n_flux
    index = jnp.where(
        present_ref[...] == 1, entry_ref[...] * n_flux + source_ref[...], jnp.full(source_ref.shape, spare, I32)
    )
    idx_v[:, LANES : LANES + n_ocean] = index
    req_v[pl.ds(tile * 8, 8), :] = wanted_ref[...]
    table[pl.ds(spare, 8), :] = jnp.zeros((8, LANES), F32)

    def tendency(s):
        hi = s.astype(BF16)
        lo = (s - hi.astype(F32)).astype(BF16)
        both = jnp.dot(vv[...], jnp.concatenate([hi, lo], axis=0), preferred_element_type=F32)
        return TIME_STEP * jnp.tanh(both[0:lev] + both[lev : 2 * lev])

    column = weight_ref[...]

    def first_steps(i):
        load_state(i).wait()
        part = pl.ds(i * chunk, chunk)
        s = state[:, part]
        s = s + tendency(s)
        s = s + tendency(s)
        state[:, part] = s
        line = jnp.sum(s * column, axis=0, keepdims=True)
        for k in range(chunk // LANES):
            fluxf[i * (chunk // LANES) + k : i * (chunk // LANES) + k + 1, :] = line[:, k * LANES : (k + 1) * LANES]

    for i in range(n_chunk - 1):
        first_steps(i)
    pl.semaphore_wait(barrier, count - 1)

    after, before = lax.rem(tile + 1, tiles), lax.rem(tile + tiles - 1, tiles)

    def halo(ref, src, dst, k, target):
        return pltpu.make_async_remote_copy(
            src_ref=ref.at[src],
            dst_ref=ref.at[dst],
            send_sem=halo_ssem.at[k],
            recv_sem=halo_rsem.at[k],
            device_id=(group, target),
            device_id_type=MESH,
        )

    everything = slice(None)
    halos = (
        halo(coef, (pl.ds(own, HALO), everything), (pl.ds(0, HALO), everything), 0, after),
        halo(coef, (pl.ds(HALO, HALO), everything), (pl.ds(HALO + own, HALO), everything), 1, before),
        halo(idx_v, (everything, pl.ds(n_ocean, LANES)), (everything, pl.ds(0, LANES)), 2, after),
        halo(idx_v, (everything, pl.ds(LANES, LANES)), (everything, pl.ds(LANES + n_ocean, LANES)), 3, before),
    )
    for copy in halos:
        copy.start()

    def request(i):
        other = lax.rem(tile + i, tiles)
        slot = pl.ds(tile * 8, 8)
        return pltpu.make_async_remote_copy(
            src_ref=req_v.at[slot],
            dst_ref=req_v.at[slot],
            send_sem=req_ssem.at[i],
            recv_sem=req_rsem.at[i],
            device_id=(group, other),
            device_id_type=MESH,
        )

    def each(make, what, first, last):
        def step(i, carry):
            what(make(i))
            return carry

        lax.fori_loop(first, last, step, 0)

    start, sent, arrived = (lambda c: c.start()), (lambda c: c.wait_send()), (lambda c: c.wait_recv())
    each(request, start, 1, tiles)

    first_steps(n_chunk - 1)
    mine = pl.ds(pl.multiple_of(me * nrows, nrows), nrows)
    flux_all[mine, :] = fluxf[...].astype(BF16)

    def flux_copy(i):
        g, t, _ = peer_of(i)
        return pltpu.make_async_remote_copy(
            src_ref=flux_all.at[mine],
            dst_ref=flux_all.at[mine],
            send_sem=flux_ssem.at[i],
            recv_sem=flux_rsem.at[i],
            device_id=(g, t),
            device_id_type=MESH,
        )

    each(flux_copy, start, 1, count)

    def store_pre(i):
        part = pl.ds(i * chunk, chunk)
        return pltpu.make_async_copy(state.at[:, part], pre_hbm.at[:, part], out_sem.at[i])

    for i in range(n_chunk):
        part = pl.ds(i * chunk, chunk)
        s = state[:, part]
        state[:, part] = s + tendency(s)
        store_pre(i).start()

    for copy in halos:
        copy.wait()
    index_copy = pltpu.make_async_copy(idx_v, idx_s, idx_sem)
    index_copy.start()
    each(request, arrived, 1, tiles)

    base = tile * n_ocean
    where_col = lax.broadcasted_iota(I32, (nrows, n_ocean), 1)
    stacked = (lax.rem(where_col, own)) * per + lax.div(where_col, own)

    def pick(t, carry):
        block = req_v[pl.ds(pl.multiple_of(t * 8, 8), 8), :]
        col = jnp.transpose(jnp.broadcast_to(block[0:1, :], (LANES, LANES)))[0:nrows, 0:1] - base
        hit = jnp.where(col == stacked, 1.0, 0.0).astype(BF16)
        picks[pl.ds(pl.multiple_of(t * nrows, nrows), nrows), :] = hit
        return carry

    lax.fori_loop(0, tiles, pick, 0)

    inner = jnp.where(coef[...] > 0.0, 1.0 / coef[...], 0.0)
    coef[...] = inner
    coef[0:HALO, :] = jnp.where(tile > 0, inner[0:HALO], 0.0)
    coef[HALO + own : ext, :] = jnp.where(tile < tiles - 1, inner[HALO + own : ext], 0.0)

    each(flux_copy, arrived, 1, count)
    rows_at_once = min(512, n_flux)

    def products(i, carry):
        at = pl.multiple_of(i * rows_at_once, rows_at_once)
        some = flux_all[pl.ds(at, rows_at_once), :]
        for b in range(0, n_block, 2):
            pair = jnp.concatenate([blocks_ref[b], blocks_ref[b + 1]], axis=1)
            got = jnp.dot(some, pair, preferred_element_type=F32)
            table[pl.ds(pl.multiple_of(b * n_flux + at, rows_at_once), rows_at_once), :] = got[:, 0:LANES]
            table[pl.ds(pl.multiple_of((b + 1) * n_flux + at, rows_at_once), rows_at_once), :] = got[:, LANES:]
        return carry

    lax.fori_loop(0, n_flux // rows_at_once, products, 0)

    index_copy.wait()
    zero_rows = jnp.zeros((HALO, width), F32)
    field[0:HALO, :] = zero_rows
    field[HALO + own : ext, :] = zero_rows

    def forcing_row(g_tile, s, j):
        e = (g_tile * 8 + s - HALO) * per + j + LANES
        total = table[pl.ds(idx_s[0, e], 1), :]
        for k in range(1, 4):
            total = total + table[pl.ds(idx_s[k, e], 1), :]
        at = pl.multiple_of(g_tile * 8, 8)
        block = field.at[pl.ds(at, 8), pl.ds(pl.multiple_of(j * LANES, LANES), LANES)]
        block[s : s + 1, :] = total

    def edge(j, carry):
        for s in (HALO - 3, HALO - 2, HALO - 1):
            forcing_row(0, s, j)
        for s in (0, 1, 2):
            forcing_row(ext // 8 - 1, s, j)
        return carry

    lax.fori_loop(0, per, edge, 0)

    def inside_rows(n, carry):
        g_tile, j = 1 + lax.div(n, per), lax.rem(n, per)
        for s in range(8):
            forcing_row(g_tile, s, j)
        return carry

    lax.fori_loop(0, own // 8 * per, inside_rows, 0)

    n_tile = ext // 8
    top = lax.broadcasted_iota(I32, (8, width), 0) == 0
    bottom = lax.broadcasted_iota(I32, (8, width), 0) == 7

    def rows8(ref, k):
        return ref[pl.ds(pl.multiple_of(k * 8, 8), 8), :]

    def beside(ref, k):
        here = rows8(ref, k)
        above = rows8(ref, jnp.maximum(k - 1, 0))
        below = rows8(ref, jnp.minimum(k + 1, n_tile - 1))
        up = jnp.where(top, pltpu.roll(above, 1, 0), pltpu.roll(here, 1, 0))
        down = jnp.where(bottom, pltpu.roll(below, 7, 0), pltpu.roll(here, 7, 0))
        return up + down + pltpu.roll(here, 1, 1) + pltpu.roll(here, width - 1, 1)

    def folded(value):
        total = value[:, 0:LANES]
        for k in range(1, per):
            total = total + value[:, k * LANES : (k + 1) * LANES]
        return total

    nothing = jnp.zeros((8, LANES), F32)

    def first(k, carry):
        f = rows8(field, k)
        w = rows8(coef, k) * f
        w0[pl.ds(pl.multiple_of(k * 8, 8), 8), :] = w
        inside = jnp.logical_and(k >= 1, k < n_tile - 1)
        return carry + jnp.where(inside, folded(w * f), 0.0)

    nu0 = lax.fori_loop(0, n_tile, first, nothing)

    def apply(w_old, w_new, k, carry):
        a, b = carry
        q = rows8(field, k) - beside(w_old, k)
        w = rows8(coef, k) * q
        field[pl.ds(pl.multiple_of(k * 8, 8), 8), :] = q
        w_new[pl.ds(pl.multiple_of(k * 8, 8), 8), :] = w
        inside = jnp.logical_and(k >= 1, k < n_tile - 1)
        a = a + jnp.where(inside, folded(rows8(w_old, k) * q), 0.0)
        b = b + jnp.where(inside, folded(w * q), 0.0)
        return a, b

    nu1, nu2 = lax.fori_loop(0, n_tile, functools.partial(apply, w0, w1), (nothing, nothing))
    nu3, nu4 = lax.fori_loop(0, n_tile, functools.partial(apply, w1, w2), (nothing, nothing))

    def last(k, carry):
        q = rows8(field, k) - beside(w2, k)
        return carry + folded(rows8(w2, k) * q)

    nu5 = lax.fori_loop(1, n_tile - 1, last, nothing)

    gram_send[...] = jnp.zeros((8, LANES), F32)
    for k, nu in enumerate((nu0, nu1, nu2, nu3, nu4, nu5)):
        gram_send[k : k + 1, :] = jnp.sum(nu, axis=0, keepdims=True)
    gram_slot = pl.ds(pl.multiple_of(tile * 8, 8), 8)
    gram_recv[gram_slot, :] = gram_send[...]

    def gram_copy(i):
        return pltpu.make_async_remote_copy(
            src_ref=gram_send,
            dst_ref=gram_recv.at[gram_slot],
            send_sem=gram_ssem.at[i],
            recv_sem=gram_rsem.at[i],
            device_id=(group, lax.rem(tile + i, tiles)),
            device_id_type=MESH,
        )

    each(gram_copy, start, 1, tiles)
    each(gram_copy, arrived, 1, tiles)
    total = jnp.sum(gram_recv[...].reshape(tiles, 8, LANES), axis=0)
    total = jnp.sum(total, axis=1, keepdims=True)
    n0, n1, n2, n3, n4, n5 = (total[k : k + 1, :] for k in range(6))

    def inverse(pivot, scale):
        good = pivot > 1e-6 * scale
        return jnp.where(good, 1.0 / jnp.where(good, pivot, 1.0), 0.0)

    i0 = inverse(n1, 0.0 * n1)
    l1, l2 = n2 * i0, n3 * i0
    d1, h = n3 - l1 * n2, n4 - l1 * n3
    i1 = inverse(d1, n3)
    l3 = h * i1
    d2 = n5 - l2 * n3 - l3 * h
    i2 = inverse(d2, n5)
    y1 = n1 - l1 * n0
    y2 = n2 - l2 * n0 - l3 * y1
    c2 = y2 * i2
    c1 = y1 * i1 - l3 * c2
    c0 = n0 * i0 - l1 * c1 - l2 * c2
    c0, c1, c2 = (jnp.broadcast_to(c, (1, width)) for c in (c0, c1, c2))

    def combine(k, carry):
        at = pl.multiple_of(k * 16, 16)
        inner_at = pl.multiple_of(HALO + k * 16, 8)
        part = pl.ds(inner_at, 16)
        x = c0 * w0[part, :] + c1 * w1[part, :] + c2 * w2[part, :]
        height[pl.ds(at, 16), :] = x
        warm = jnp.where(mask_ref[pl.ds(at, 16), :] == 1, temp_ref[pl.ds(at, 16), :] + x, 0.0).astype(BF16)
        for j in range(per):
            sst[pl.ds(pl.multiple_of(j * own + k * 16, 16), 16), :] = warm[:, j * LANES : (j + 1) * LANES]
        return carry

    lax.fori_loop(0, own // 16, combine, 0)
    height_copy = pltpu.make_async_copy(height, height_hbm, height_sem)
    height_copy.start()

    n_req = tiles * nrows
    at_once = min(256, n_req)

    def picked(i, carry):
        part = pl.ds(pl.multiple_of(i * at_once, at_once), at_once)
        rows_send[part, :] = jnp.dot(picks[part, :], sst[...], preferred_element_type=F32).astype(BF16)
        return carry

    lax.fori_loop(0, n_req // at_once, picked, 0)
    rows_slot = pl.ds(pl.multiple_of(tile * nrows, nrows), nrows)
    rows_recv[rows_slot, :] = rows_send[rows_slot, :]

    def rows_copy(i):
        other = lax.rem(tile + i, tiles)
        return pltpu.make_async_remote_copy(
            src_ref=rows_send.at[pl.ds(pl.multiple_of(other * nrows, nrows), nrows)],
            dst_ref=rows_recv.at[rows_slot],
            send_sem=rows_ssem.at[i],
            recv_sem=rows_rsem.at[i],
            device_id=(group, other),
            device_id_type=MESH,
        )

    each(rows_copy, start, 1, tiles)
    each(rows_copy, arrived, 1, tiles)
    got = jnp.sum(rows_recv[...].astype(F32).reshape(tiles, nrows, LANES), axis=0)
    for k in range(nrows):
        rows_out[:, k * LANES : (k + 1) * LANES] = got[k : k + 1, :]

    each(request, sent, 1, tiles)
    each(flux_copy, sent, 1, count)
    each(gram_copy, sent, 1, tiles)
    each(rows_copy, sent, 1, tiles)
    for i in range(n_chunk):
        store_pre(i).wait()
    height_copy.wait()


def solution(mesh):
    groups, tiles = mesh.shape["comp"], mesh.shape["tile"]
    count = groups * tiles

    def body(state, vco, weight, response, blocks, source, entry, present, mask, depth, temp, wanted):
        lev, cols = state.shape
        own, width = mask.shape
        nrows = cols // LANES
        n_flux = count * nrows
        n_ocean = own * width // LANES
        ext = own + 2 * HALO
        n_req = tiles * nrows
        n_chunk = max(1, cols // 1024)
        vmem = pl.BlockSpec(memory_space=pltpu.VMEM)
        anywhere = pl.BlockSpec(memory_space=pl.ANY)
        dma = pltpu.SemaphoreType.DMA
        asked = jnp.broadcast_to(jnp.pad(wanted, (0, LANES - nrows), constant_values=-1)[None, :], (8, LANES))
        pre, height, rows = pl.pallas_call(
            functools.partial(kernel, groups, tiles),
            out_shape=(
                jax.ShapeDtypeStruct((lev, cols), F32),
                jax.ShapeDtypeStruct((own, width), F32),
                jax.ShapeDtypeStruct((1, cols), F32),
            ),
            in_specs=[anywhere] + [vmem] * 10,
            out_specs=(anywhere, anywhere, vmem),
            scratch_shapes=[
                pltpu.VMEM((lev, cols), F32),
                pltpu.VMEM((2 * lev, 2 * lev), BF16),
                pltpu.VMEM((nrows, LANES), F32),
                pltpu.VMEM((n_flux, LANES), BF16),
                pltpu.VMEM((blocks.shape[0] * n_flux + 8, LANES), F32),
                pltpu.VMEM((4, n_ocean + 2 * LANES), I32),
                pltpu.SMEM((4, n_ocean + 2 * LANES), I32),
                pltpu.VMEM((ext, width), F32),
                pltpu.VMEM((ext, width), F32),
                pltpu.VMEM((ext, width), F32),
                pltpu.VMEM((ext, width), F32),
                pltpu.VMEM((ext, width), F32),
                pltpu.VMEM((own, width), F32),
                pltpu.VMEM((tiles * 8, LANES), I32),
                pltpu.VMEM((n_req, n_ocean), BF16),
                pltpu.VMEM((n_ocean, LANES), BF16),
                pltpu.VMEM((n_req, LANES), BF16),
                pltpu.VMEM((n_req, LANES), BF16),
                pltpu.VMEM((8, LANES), F32),
                pltpu.VMEM((tiles * 8, LANES), F32),
                dma((n_chunk,)),
                dma((n_chunk,)),
                dma,
                dma,
                dma((count,)),
                dma((count,)),
                dma((tiles,)),
                dma((tiles,)),
                dma((4,)),
                dma((4,)),
                dma((tiles,)),
                dma((tiles,)),
                dma((tiles,)),
                dma((tiles,)),
            ],
            compiler_params=pltpu.CompilerParams(
                collective_id=0, has_side_effects=True, vmem_limit_bytes=48 * 1024 * 1024
            ),
        )(
            state,
            vco,
            weight.reshape(lev, 1),
            blocks,
            source.T,
            entry.T,
            present.T,
            mask,
            depth,
            temp,
            asked,
        )
        return pre + (TIME_STEP * response)[:, None] * rows, height

    split = P(None, ("comp", "tile"))
    ocean = P("tile", None)
    return jax.shard_map(
        body,
        mesh=mesh,
        in_specs=(split, P(), P(), P(), P(), ocean, ocean, ocean, ocean, ocean, ocean, P(("comp", "tile"))),
        out_specs=(split, ocean),
        check_vma=False,
    )
```

profile of v0, /device:TPU:1, one launch (start us, length us, event | category | flops | bytes accessed | tf_op | source)
XLA Modules:
  0.0 81.3 jit_solution(14361268431775553695)
XLA Ops:
  0.6 0.7 broadcast_multiply_fusion
  1.3 0.7 pad.4
  2.0 0.8 copy.14.weight_ref
  2.7 0.0 copy-start
  2.7 1.1 %copy-done = s32[64,2560]{1,0:T(8,128)S(1)} copy-done((s32[64,2560]{1,0:T(8,128)S(1)}, s32[64,2560]{1,0:T(8,128)}, u32[]{:S(2)}) %copy-start) | copy-done | bytes 655384
  3.8 0.0 copy-start.1
  3.8 1.1 %copy-done.1 = f32[64,2560]{1,0:T(8,128)S(1)} copy-done((f32[64,2560]{1,0:T(8,128)S(1)}, f32[64,2560]{1,0:T(8,128)}, u32[]{:S(2)}) %copy-start.1) | copy-done | bytes 655384
  4.9 0.0 copy-start.2
  4.9 1.1 %copy-done.2 = f32[64,2560]{1,0:T(8,128)S(1)} copy-done((f32[64,2560]{1,0:T(8,128)S(1)}, f32[64,2560]{1,0:T(8,128)}, u32[]{:S(2)}) %copy-start.2) | copy-done | bytes 655384
  6.0 0.0 copy-start.3
  6.0 0.9 %copy-done.3 = bf16[8,128,128]{2,1,0:T(8,128)(2,1)S(1)} copy-done((bf16[8,128,128]{2,1,0:T(8,128)(2,1)S(1)}, bf16[8,128,128]{2,1,0:T(8,128)(2,1)}, u32[]{:S(2)}) %copy-start.3) | copy-done | bytes 262168
  6.9 0.0 copy-start.4
  6.9 0.8 %copy-done.4 = f32[128,128]{1,0:T(8,128)S(1)} copy-done((f32[128,128]{1,0:T(8,128)S(1)}, f32[128,128]{1,0:T(8,128)}, u32[]{:S(2)}) %copy-start.4) | copy-done | bytes 65560
  7.8 0.0 copy-start.5
  7.8 0.7 copy-done.5
  8.5 0.0 copy-start.6
  8.5 0.7 copy-done.6
  9.2 0.0 copy-start.7
  9.2 0.7 copy-done.7
  10.0 68.9 %shard_map.131 = (f32[128,4096]{1,0:T(8,128)S(1)}, f32[64,2560]{1,0:T(8,128)S(1)}, f32[1,4096]{1,0:T(1,128)S(1)}) custom-call(f32[128,4096]{1,0:T(8,128)} %state_hbm.1, f32[128,128]{1,0:T(8,128)S(1)} %copy-done.4, f32[128,1]{1,0:T(8,128)S(1)} %copy.14.weight_ref, bf16[8,128,128]{2,1,0:T(8,128)(2,1)S(1)} %copy-done.3, s32[4,1280]{1,0:T(4,128)S(1)} %bitcast.5, ...), custom_call_target="tpu_custom_call" | custom-call | tf_op jit(solution)/shard_map/pallas_call | solution.py:448
  78.8 1.6 %multiply_add_fusion = f32[128,4096]{1,0:T(8,128)} fusion(f32[128,4096]{1,0:T(8,128)S(1)} %get-tuple-element.5, f32[4096]{0:T(1024)S(1)} %bitcast.8, f32[128]{0:T(128)S(1)} %broadcast_multiply_fusion), kind=kLoop, calls=%fused_computation | loop fusion | flops 1048576 | bytes 4211200 | tf_op jit(solution)/shard_map/add | solution.py:509
  80.4 0.8 %copy.16 = f32[64,2560]{1,0:T(8,128)} copy(f32[64,2560]{1,0:T(8,128)S(1)} %get-tuple-element.11) | data formatting | bytes 1310720
  (1 shorter events, 0.0 us)
Async XLA Ops:
  2.7 1.1 %copy-start = (s32[64,2560]{1,0:T(8,128)S(1)}, s32[64,2560]{1,0:T(8,128)}, u32[]{:S(2)}) copy-start(s32[64,2560]{1,0:T(8,128)} %mask_ref.1) | copy-start | bytes 1966084
  3.8 1.1 %copy-start.1 = (f32[64,2560]{1,0:T(8,128)S(1)}, f32[64,2560]{1,0:T(8,128)}, u32[]{:S(2)}) copy-start(f32[64,2560]{1,0:T(8,128)} %depth_ref.1) | copy-start | bytes 1966084
  4.9 1.1 %copy-start.2 = (f32[64,2560]{1,0:T(8,128)S(1)}, f32[64,2560]{1,0:T(8,128)}, u32[]{:S(2)}) copy-start(f32[64,2560]{1,0:T(8,128)} %temp_ref.1) | copy-start | bytes 1966084
  6.0 0.9 %copy-start.3 = (bf16[8,128,128]{2,1,0:T(8,128)(2,1)S(1)}, bf16[8,128,128]{2,1,0:T(8,128)(2,1)}, u32[]{:S(2)}) copy-start(bf16[8,128,128]{2,1,0:T(8,128)(2,1)} %blocks_ref.1) | copy-start | bytes 786436
  6.9 0.8 %copy-start.4 = (f32[128,128]{1,0:T(8,128)S(1)}, f32[128,128]{1,0:T(8,128)}, u32[]{:S(2)}) copy-start(f32[128,128]{1,0:T(8,128)} %vco_ref.1) | copy-start | bytes 196612
  7.8 0.7 copy-start.5
  8.5 0.7 copy-start.6
  9.2 0.7 copy-start.7
where the time goes:
time: 81.8 us; the launch traced here: 81.3 us
  Pallas kernels  68.9 us (84%)
  local copies, waits for them, and re-layouts  9.48 us (12%)
  other arithmetic  2.26 us (3%)
    pallas_call x1, Pallas kernels, body(): pl.pallas_call(functools.partial(kernel, groups, tiles), out_shape=(jax.S...  68.9 us
    unnamed x17, local copies, waits for them, and re-layouts  8.06 us

commit v1 on v0

v1 whole, which is shorter than its diff:
```python
import functools

import jax
import jax.numpy as jnp
from jax import lax
from jax.experimental import pallas as pl
from jax.experimental.pallas import tpu as pltpu
from jax.sharding import PartitionSpec as P

F32, BF16, I32 = jnp.float32, jnp.bfloat16, jnp.int32
MESH = pl.DeviceIdType.MESH
LANES = 128
HALO = 8
TIME_STEP = 0.5


def kernel(
    groups,
    tiles,
    state_hbm,
    vco_hbm,
    weight_hbm,
    blocks_hbm,
    source_hbm,
    entry_hbm,
    present_hbm,
    mask_hbm,
    depth_hbm,
    temp_hbm,
    wanted_hbm,
    pre,
    height,
    rows_out,
    state,
    vco_ref,
    weight_ref,
    blocks_ref,
    source_ref,
    entry_ref,
    present_ref,
    mask_ref,
    depth_ref,
    temp_ref,
    wanted_ref,
    vv,
    fluxf,
    flux_all,
    table,
    idx_v,
    idx_s,
    coef,
    field,
    w0,
    w1,
    w2,
    req_v,
    picks,
    sst,
    rows_send,
    rows_recv,
    gram_send,
    gram_recv,
    in_sem,
    load_sem,
    idx_sem,
    flux_ssem,
    flux_rsem,
    fwd_ssem,
    fwd_rsem,
    req_ssem,
    req_rsem,
    halo_ssem,
    halo_rsem,
    gram_ssem,
    gram_rsem,
    rows_ssem,
    rows_rsem,
):
    group, tile = lax.axis_index("comp"), lax.axis_index("tile")
    count = groups * tiles
    lev, cols = state.shape
    own, width = mask_hbm.shape
    per = width // LANES
    ext = own + 2 * HALO
    nrows = cols // LANES
    n_flux = count * nrows
    n_entry, n_ocean = source_hbm.shape
    n_block = blocks_ref.shape[0]
    chunk = min(1024, cols)
    n_chunk = cols // chunk
    core, side = lax.rem(tile, 2), tiles // 2
    n_chip = groups * side
    chip = group * side + lax.div(tile, 2)
    partner = tile + 1 - 2 * core
    half = n_flux // 2
    part_rows = side * nrows
    span = n_ocean + 2 * LANES

    def chip_peer(i):
        other = lax.rem(chip + i, n_chip)
        return lax.div(other, side), 2 * lax.rem(other, side) + core

    loads = {
        name: pltpu.make_async_copy(source, target, load_sem.at[i])
        for i, (name, source, target) in enumerate(
            (
                ("vco", vco_hbm, vco_ref),
                ("weight", weight_hbm, weight_ref),
                ("mask", mask_hbm, mask_ref),
                ("depth", depth_hbm, depth_ref),
                ("source", source_hbm, source_ref),
                ("entry", entry_hbm, entry_ref),
                ("present", present_hbm, present_ref),
                ("wanted", wanted_hbm, wanted_ref),
                ("blocks", blocks_hbm, blocks_ref),
                ("temp", temp_hbm, temp_ref),
            )
        )
    }
    loads["vco"].start()

    def load_state(i):
        part = pl.ds(i * chunk, chunk)
        return pltpu.make_async_copy(state_hbm.at[:, part], state.at[:, part], in_sem.at[i])

    for i in range(n_chunk):
        load_state(i).start()

    barrier = pltpu.get_barrier_semaphore()

    def greet(target):
        pl.semaphore_signal(barrier, inc=1, device_id=target, device_id_type=MESH)

    def greet_chip(i, carry):
        greet(chip_peer(i))
        return carry

    def greet_other_core(i, carry):
        greet((group, 2 * i + 1 - core))
        return carry

    lax.fori_loop(1, n_chip, greet_chip, 0)
    lax.fori_loop(0, side, greet_other_core, 0)
    for name in loads:
        if name != "vco":
            loads[name].start()

    loads["vco"].wait()
    vco = vco_ref[...]
    v_hi = vco.astype(BF16)
    v_lo = (vco - v_hi.astype(F32)).astype(BF16)
    vv[0:lev, 0:lev] = v_hi
    vv[0:lev, lev : 2 * lev] = v_hi
    vv[lev : 2 * lev, 0:lev] = v_lo
    vv[lev : 2 * lev, lev : 2 * lev] = v_lo

    def tendency(s):
        hi = s.astype(BF16)
        lo = (s - hi.astype(F32)).astype(BF16)
        both = jnp.dot(vv[...], jnp.concatenate([hi, lo], axis=0), preferred_element_type=F32)
        return TIME_STEP * jnp.tanh(both[0:lev] + both[lev : 2 * lev])

    loads["weight"].wait()
    column = jnp.transpose(jnp.broadcast_to(weight_ref[...], (LANES, lev)))[:, 0:1]

    def first_steps(i):
        load_state(i).wait()
        part = pl.ds(i * chunk, chunk)
        s = state[:, part]
        s = s + tendency(s)
        s = s + tendency(s)
        state[:, part] = s
        line = jnp.sum(s * column, axis=0, keepdims=True)
        for k in range(chunk // LANES):
            fluxf[i * (chunk // LANES) + k : i * (chunk // LANES) + k + 1, :] = line[:, k * LANES : (k + 1) * LANES]

    for i in range(n_chunk - 1):
        first_steps(i)

    for name in ("mask", "depth", "source", "entry", "present", "wanted"):
        loads[name].wait()
    mask = mask_ref[...].astype(F32)
    coef[HALO : HALO + own, :] = mask * (4.0 + depth_ref[...])
    spare = n_block * n_flux
    source = source_ref[...]
    holder = lax.div(source, nrows)
    row = lax.rem(holder, 2) * half + lax.div(holder, 2) * nrows + lax.rem(source, nrows)
    index = jnp.where(present_ref[...] == 1, entry_ref[...] * n_flux + row, jnp.full(source.shape, spare, I32))
    for k in range(n_entry):
        idx_v[k, :, LANES : LANES + n_ocean] = index[k : k + 1, :]
    own_slot = pl.ds(pl.multiple_of(tile * 8, 8), 8)
    req_v[own_slot, :] = jnp.full((8, LANES), -1, I32)
    req_v[own_slot, 0:nrows] = jnp.broadcast_to(wanted_ref[...], (8, nrows))
    table[pl.ds(spare, 8), :] = jnp.zeros((8, LANES), F32)

    pl.semaphore_wait(barrier, n_chip - 1 + side)

    start = lambda c: c.start()

    def each(make, what, first, last):
        def step(i, carry):
            what(make(i))
            return carry

        lax.fori_loop(first, last, step, 0)

    def many(ref, rows, send_sem, recv_sem):
        return pltpu.make_async_remote_copy(
            src_ref=ref.at[pl.ds(0, rows)],
            dst_ref=ref.at[pl.ds(0, rows)],
            send_sem=send_sem,
            recv_sem=recv_sem,
            device_id=(group, partner),
            device_id_type=MESH,
        )

    def request(i):
        return pltpu.make_async_remote_copy(
            src_ref=req_v.at[own_slot],
            dst_ref=req_v.at[own_slot],
            send_sem=req_ssem,
            recv_sem=req_rsem,
            device_id=(group, lax.rem(tile + i, tiles)),
            device_id_type=MESH,
        )

    each(request, start, 1, tiles)
    requests = many(req_v, (tiles - 1) * 8, req_ssem, req_rsem)

    first_steps(n_chunk - 1)
    mine = pl.ds(pl.multiple_of(core * half + chip * nrows, nrows), nrows)
    flux_all[mine, :] = fluxf[...].astype(BF16)

    def flux_copy(i):
        return pltpu.make_async_remote_copy(
            src_ref=flux_all.at[mine],
            dst_ref=flux_all.at[mine],
            send_sem=flux_ssem,
            recv_sem=flux_rsem.at[group],
            device_id=chip_peer(i),
            device_id_type=MESH,
        )

    each(flux_copy, start, 1, n_chip)

    after, before = lax.rem(tile + 1, tiles), lax.rem(tile + tiles - 1, tiles)

    def halo(ref, src, dst, k, target):
        return pltpu.make_async_remote_copy(
            src_ref=ref.at[src],
            dst_ref=ref.at[dst],
            send_sem=halo_ssem.at[k],
            recv_sem=halo_rsem.at[k],
            device_id=(group, target),
            device_id_type=MESH,
        )

    everything = slice(None)
    halos = (
        halo(coef, (pl.ds(own, HALO), everything), (pl.ds(0, HALO), everything), 0, after),
        halo(coef, (pl.ds(HALO, HALO), everything), (pl.ds(HALO + own, HALO), everything), 1, before),
        halo(idx_v, (everything, everything, pl.ds(n_ocean, LANES)), (everything, everything, pl.ds(0, LANES)), 2, after),
        halo(
            idx_v,
            (everything, everything, pl.ds(LANES, LANES)),
            (everything, everything, pl.ds(LANES + n_ocean, LANES)),
            3,
            before,
        ),
    )
    for copy in halos:
        copy.start()

    for i in range(n_chunk):
        part = pl.ds(i * chunk, chunk)
        s = state[:, part]
        pre[:, part] = s + tendency(s)

    requests.wait_recv()
    asked = jnp.concatenate([req_v[8 * t : 8 * t + 1, :] for t in range(tiles)], axis=0)
    asked = jnp.concatenate([asked - tile * n_ocean, jnp.zeros((LANES - tiles, LANES), I32)], axis=0)
    asked = jnp.transpose(asked)
    where_col = lax.broadcasted_iota(I32, (nrows, n_ocean), 1)
    stacked = lax.rem(where_col, own) * per + lax.div(where_col, own)
    for t in range(tiles):
        hit = asked[0:nrows, t : t + 1] == stacked
        picks[t * nrows : (t + 1) * nrows, :] = jnp.where(hit, 1.0, 0.0).astype(BF16)

    loads["blocks"].wait()
    pairs = [jnp.concatenate([blocks_ref[b], blocks_ref[b + 1]], axis=1) for b in range(0, n_block, 2)]

    def products(at):
        some = flux_all[pl.ds(pl.multiple_of(at, part_rows), part_rows), :]
        for b, pair in enumerate(pairs):
            got = jnp.dot(some, pair, preferred_element_type=F32)
            for k in range(2):
                to = pl.multiple_of((2 * b + k) * n_flux + at, part_rows)
                table[pl.ds(to, part_rows), :] = got[:, k * LANES : (k + 1) * LANES]

    def forward(g):
        slot = pl.ds(pl.multiple_of(core * half + g * part_rows, part_rows), part_rows)
        return pltpu.make_async_remote_copy(
            src_ref=flux_all.at[slot],
            dst_ref=flux_all.at[slot],
            send_sem=fwd_ssem.at[g],
            recv_sem=fwd_rsem.at[g],
            device_id=(group, partner),
            device_id_type=MESH,
        )

    order = [0] + [k for n in range(1, groups // 2 + 1) for k in sorted({n, groups - n})]
    for n, offset in enumerate(order):
        g = lax.rem(group + offset, groups)
        blocks_in = side - 1 if offset == 0 else side
        many(flux_all, blocks_in * nrows, flux_ssem, flux_rsem.at[g]).wait_recv()
        forward(g).start()
        products(core * half + g * part_rows)
        if n > 0:
            late = lax.rem(group + order[n - 1], groups)
            forward(late).wait_recv()
            products((1 - core) * half + late * part_rows)
        if n == len(order) - 2:
            for copy in halos:
                copy.wait()
            index_copies = [
                pltpu.make_async_copy(
                    idx_v.at[k, 0], idx_s.at[pl.ds(k * span, span)], idx_sem.at[k]
                )
                for k in range(n_entry)
            ]
            for copy in index_copies:
                copy.start()
            inner = jnp.where(coef[...] > 0.0, 1.0 / coef[...], 0.0)
            coef[...] = inner
            coef[0:HALO, :] = jnp.where(tile > 0, inner[0:HALO], 0.0)
            coef[HALO + own : ext, :] = jnp.where(tile < tiles - 1, inner[HALO + own : ext], 0.0)
            zero_rows = jnp.zeros((HALO, width), F32)
            field[0:HALO, :] = zero_rows
            field[HALO + own : ext, :] = zero_rows
            for copy in index_copies:
                copy.wait()
    late = lax.rem(group + order[-1], groups)
    forward(late).wait_recv()
    products((1 - core) * half + late * part_rows)

    def forcing_rows(g_tile, j, rows):
        base = g_tile * 8 * per + j
        totals = []
        for s in rows:
            e = base + ((s - HALO) * per + LANES)
            got = [table[pl.ds(idx_s[e + k * span], 1), :] for k in range(n_entry)]
            while len(got) > 1:
                got = [sum(got[k : k + 2][1:], got[k]) for k in range(0, len(got), 2)]
            totals.append(got[0])
        at = pl.multiple_of(g_tile * 8, 8)
        block = field.at[pl.ds(at, 8), pl.ds(pl.multiple_of(j * LANES, LANES), LANES)]
        for s, total in zip(rows, totals):
            block[s : s + 1, :] = total

    def edge(j, carry):
        forcing_rows(0, j, (HALO - 3, HALO - 2, HALO - 1))
        forcing_rows(ext // 8 - 1, j, (0, 1, 2))
        return carry

    lax.fori_loop(0, per, edge, 0)

    def inside_rows(n, carry):
        forcing_rows(1 + lax.div(n, per), lax.rem(n, per), range(8))
        return carry

    lax.fori_loop(0, own // 8 * per, inside_rows, 0, unroll=2)

    n_tile = ext // 8
    top = lax.broadcasted_iota(I32, (8, width), 0) == 0
    bottom = lax.broadcasted_iota(I32, (8, width), 0) == 7

    def rows8(ref, k):
        return ref[pl.ds(pl.multiple_of(k * 8, 8), 8), :]

    def beside(ref, k):
        here = rows8(ref, k)
        above = rows8(ref, jnp.maximum(k - 1, 0))
        below = rows8(ref, jnp.minimum(k + 1, n_tile - 1))
        up = jnp.where(top, pltpu.roll(above, 1, 0), pltpu.roll(here, 1, 0))
        down = jnp.where(bottom, pltpu.roll(below, 7, 0), pltpu.roll(here, 7, 0))
        return up + down + pltpu.roll(here, 1, 1) + pltpu.roll(here, width - 1, 1)

    def folded(value):
        total = value[:, 0:LANES]
        for k in range(1, per):
            total = total + value[:, k * LANES : (k + 1) * LANES]
        return total

    nothing = jnp.zeros((8, LANES), F32)

    def first(k, carry):
        f = rows8(field, k)
        w = rows8(coef, k) * f
        w0[pl.ds(pl.multiple_of(k * 8, 8), 8), :] = w
        inside = jnp.logical_and(k >= 1, k < n_tile - 1)
        return carry + jnp.where(inside, folded(w * f), 0.0)

    nu0 = lax.fori_loop(0, n_tile, first, nothing, unroll=5)

    def apply(w_old, w_new, k, carry):
        a, b = carry
        q = rows8(field, k) - beside(w_old, k)
        w = rows8(coef, k) * q
        field[pl.ds(pl.multiple_of(k * 8, 8), 8), :] = q
        w_new[pl.ds(pl.multiple_of(k * 8, 8), 8), :] = w
        inside = jnp.logical_and(k >= 1, k < n_tile - 1)
        a = a + jnp.where(inside, folded(rows8(w_old, k) * q), 0.0)
        b = b + jnp.where(inside, folded(w * q), 0.0)
        return a, b

    nu1, nu2 = lax.fori_loop(0, n_tile, functools.partial(apply, w0, w1), (nothing, nothing), unroll=5)
    nu3, nu4 = lax.fori_loop(0, n_tile, functools.partial(apply, w1, w2), (nothing, nothing), unroll=5)

    def last(k, carry):
        q = rows8(field, k) - beside(w2, k)
        return carry + folded(rows8(w2, k) * q)

    nu5 = lax.fori_loop(1, n_tile - 1, last, nothing, unroll=4)

    gram_send[...] = jnp.zeros((8, LANES), F32)
    for k, nu in enumerate((nu0, nu1, nu2, nu3, nu4, nu5)):
        gram_send[k : k + 1, :] = jnp.sum(nu, axis=0, keepdims=True)
    gram_slot = pl.ds(pl.multiple_of(tile * 8, 8), 8)
    gram_recv[gram_slot, :] = gram_send[...]

    def gram_copy(i):
        return pltpu.make_async_remote_copy(
            src_ref=gram_send,
            dst_ref=gram_recv.at[gram_slot],
            send_sem=gram_ssem,
            recv_sem=gram_rsem,
            device_id=(group, lax.rem(tile + i, tiles)),
            device_id_type=MESH,
        )

    each(gram_copy, start, 1, tiles)
    gram_all = many(gram_recv, (tiles - 1) * 8, gram_ssem, gram_rsem)
    gram_all.wait_recv()
    total = jnp.sum(gram_recv[...].reshape(tiles, 8, LANES), axis=0)
    total = jnp.sum(total, axis=1, keepdims=True)
    n0, n1, n2, n3, n4, n5 = (total[k : k + 1, :] for k in range(6))

    def inverse(pivot, scale):
        good = pivot > 1e-6 * scale
        return jnp.where(good, 1.0 / jnp.where(good, pivot, 1.0), 0.0)

    i0 = inverse(n1, 0.0 * n1)
    l1, l2 = n2 * i0, n3 * i0
    d1, h = n3 - l1 * n2, n4 - l1 * n3
    i1 = inverse(d1, n3)
    l3 = h * i1
    d2 = n5 - l2 * n3 - l3 * h
    i2 = inverse(d2, n5)
    y1 = n1 - l1 * n0
    y2 = n2 - l2 * n0 - l3 * y1
    c2 = y2 * i2
    c1 = y1 * i1 - l3 * c2
    c0 = n0 * i0 - l1 * c1 - l2 * c2
    c0, c1, c2 = (jnp.broadcast_to(c, (1, width)) for c in (c0, c1, c2))

    def combine(k, carry):
        at = pl.multiple_of(k * 16, 16)
        inner_at = pl.multiple_of(HALO + k * 16, 8)
        part = pl.ds(inner_at, 16)
        x = c0 * w0[part, :] + c1 * w1[part, :] + c2 * w2[part, :]
        height[pl.ds(at, 16), :] = x
        warm = jnp.where(mask_ref[pl.ds(at, 16), :] == 1, temp_ref[pl.ds(at, 16), :] + x, 0.0).astype(BF16)
        for j in range(per):
            sst[pl.ds(pl.multiple_of(j * own + k * 16, 16), 16), :] = warm[:, j * LANES : (j + 1) * LANES]
        return carry

    loads["temp"].wait()
    lax.fori_loop(0, own // 16, combine, 0)

    n_req = tiles * nrows
    at_once = min(256, n_req)

    def picked(i, carry):
        part = pl.ds(pl.multiple_of(i * at_once, at_once), at_once)
        rows_send[part, :] = jnp.dot(picks[part, :], sst[...], preferred_element_type=F32).astype(BF16)
        return carry

    lax.fori_loop(0, n_req // at_once, picked, 0)
    rows_slot = pl.ds(pl.multiple_of(tile * nrows, nrows), nrows)
    rows_recv[rows_slot, :] = rows_send[rows_slot, :]

    def rows_copy(i):
        other = lax.rem(tile + i, tiles)
        return pltpu.make_async_remote_copy(
            src_ref=rows_send.at[pl.ds(pl.multiple_of(other * nrows, nrows), nrows)],
            dst_ref=rows_recv.at[rows_slot],
            send_sem=rows_ssem,
            recv_sem=rows_rsem,
            device_id=(group, other),
            device_id_type=MESH,
        )

    each(rows_copy, start, 1, tiles)
    rows_all = many(rows_recv, (tiles - 1) * nrows, rows_ssem, rows_rsem)
    rows_all.wait_recv()
    got = jnp.sum(rows_recv[...].astype(F32).reshape(tiles, nrows, LANES), axis=0)
    for k in range(nrows):
        rows_out[:, k * LANES : (k + 1) * LANES] = got[k : k + 1, :]

    requests.wait_send()
    many(flux_all, (n_chip - 1) * nrows, flux_ssem, flux_rsem.at[0]).wait_send()
    for g in range(groups):
        forward(g).wait_send()
    gram_all.wait_send()
    rows_all.wait_send()


def finish(pre, height, rows, response, atm_hbm, height_hbm, held, sems, height_sem):
    copy = pltpu.make_async_copy(height, height_hbm, height_sem)
    copy.start()
    lev, cols = pre.shape
    column = TIME_STEP * jnp.transpose(jnp.broadcast_to(response[...], (LANES, lev)))[:, 0:1]
    n_part = sems.shape[0]
    size = cols // n_part
    outs = []
    for i in range(n_part):
        part = pl.ds(i * size, size)
        held[:, part] = pre[:, part] + column * rows[:, part]
        outs.append(pltpu.make_async_copy(held.at[:, part], atm_hbm.at[:, part], sems.at[i]))
        outs[-1].start()
    for out in outs:
        out.wait()
    copy.wait()


def solution(mesh):
    groups, tiles = mesh.shape["comp"], mesh.shape["tile"]
    count = groups * tiles

    def body(state, vco, weight, response, blocks, source, entry, present, mask, depth, temp, wanted):
        lev, cols = state.shape
        own, width = mask.shape
        nrows = cols // LANES
        n_flux = count * nrows
        n_ocean = own * width // LANES
        ext = own + 2 * HALO
        n_req = tiles * nrows
        n_chunk = max(1, cols // 1024)
        vmem = pl.BlockSpec(memory_space=pltpu.VMEM)
        n_block, n_entry = blocks.shape[0], source.shape[1]
        anywhere = pl.BlockSpec(memory_space=pltpu.HBM)
        dma = pltpu.SemaphoreType.DMA
        pre, height, rows = pl.pallas_call(
            functools.partial(kernel, groups, tiles),
            out_shape=(
                jax.ShapeDtypeStruct((lev, cols), F32),
                jax.ShapeDtypeStruct((own, width), F32),
                jax.ShapeDtypeStruct((1, cols), F32),
            ),
            in_specs=[anywhere] * 11,
            out_specs=(vmem, vmem, vmem),
            scratch_shapes=[
                pltpu.VMEM((lev, cols), F32),
                pltpu.VMEM((lev, lev), F32),
                pltpu.VMEM((1, lev), F32),
                pltpu.VMEM((n_block, LANES, LANES), BF16),
                pltpu.VMEM((n_entry, n_ocean), I32),
                pltpu.VMEM((n_entry, n_ocean), I32),
                pltpu.VMEM((n_entry, n_ocean), I32),
                pltpu.VMEM((own, width), I32),
                pltpu.VMEM((own, width), F32),
                pltpu.VMEM((own, width), F32),
                pltpu.VMEM((1, nrows), I32),
                pltpu.VMEM((2 * lev, 2 * lev), BF16),
                pltpu.VMEM((nrows, LANES), F32),
                pltpu.VMEM((n_flux, LANES), BF16),
                pltpu.VMEM((n_block * n_flux + 8, LANES), F32),
                pltpu.VMEM((n_entry, 1, n_ocean + 2 * LANES), I32),
                pltpu.SMEM((n_entry * (n_ocean + 2 * LANES),), I32),
                pltpu.VMEM((ext, width), F32),
                pltpu.VMEM((ext, width), F32),
                pltpu.VMEM((ext, width), F32),
                pltpu.VMEM((ext, width), F32),
                pltpu.VMEM((ext, width), F32),
                pltpu.VMEM((tiles * 8, LANES), I32),
                pltpu.VMEM((n_req, n_ocean), BF16),
                pltpu.VMEM((n_ocean, LANES), BF16),
                pltpu.VMEM((n_req, LANES), BF16),
                pltpu.VMEM((n_req, LANES), BF16),
                pltpu.VMEM((8, LANES), F32),
                pltpu.VMEM((tiles * 8, LANES), F32),
                dma((n_chunk,)),
                dma((10,)),
                dma((n_entry,)),
                dma,
                dma((groups,)),
                dma((groups,)),
                dma((groups,)),
                dma,
                dma,
                dma((4,)),
                dma((4,)),
                dma,
                dma,
                dma,
                dma,
            ],
            compiler_params=pltpu.CompilerParams(
                collective_id=0, has_side_effects=True, vmem_limit_bytes=48 * 1024 * 1024
            ),
        )(
            *(
                pltpu.with_memory_space_constraint(value, pltpu.HBM)
                for value in (
                    state,
                    vco,
                    weight[None, :],
                    blocks,
                    source.T,
                    entry.T,
                    present.T,
                    mask,
                    depth,
                    temp,
                    wanted[None, :],
                )
            )
        )
        return pl.pallas_call(
            finish,
            out_shape=(jax.ShapeDtypeStruct((lev, cols), F32), jax.ShapeDtypeStruct((own, width), F32)),
            in_specs=[vmem] * 4,
            out_specs=(anywhere, anywhere),
            scratch_shapes=[pltpu.VMEM((lev, cols), F32), dma((n_chunk,)), dma],
            compiler_params=pltpu.CompilerParams(vmem_limit_bytes=16 * 1024 * 1024),
        )(pre, height, rows, response[None, :])

    split = P(None, ("comp", "tile"))
    ocean = P("tile", None)
    return jax.shard_map(
        body,
        mesh=mesh,
        in_specs=(split, P(), P(), P(), P(), ocean, ocean, ocean, ocean, ocean, ocean, P(("comp", "tile"))),
        out_specs=(split, ocean),
        check_vma=False,
    )
```

time: 81.8 us -> 50.3 us (0.61)
  Pallas kernels: 68.9 us -> 49.5 us
  local copies, waits for them, and re-layouts: 9.48 us -> 0.01 us
  other arithmetic: 2.26 us -> 0 us
    pallas_call x1, Pallas kernels: 68.9 us -> 47.8 us  [body(): pl.pallas_call(functools.partial(kernel, groups, tiles), out_shape=(jax.S...]
    unnamed x17 -> x2, local copies, waits for them, and re-layouts: 8.06 us -> 0.01 us
    pallas_call x0 -> x1, Pallas kernels: none -> 1.66 us  [body(): pl.pallas_call(finish, out_shape=(jax.ShapeDtypeStruct((lev, cols), F32),...]
    add x1 -> x0, other arithmetic: 1.6 us -> none  [body(): return (pre + (TIME_STEP * response)[:, None] * rows, height)]
where the time goes in v1:
time: 50.3 us; the launch traced here: 50.2 us
  Pallas kernels  49.5 us (98%)
  between operations  0.66 us (1%)
    pallas_call x1, Pallas kernels, body(): pl.pallas_call(functools.partial(kernel, groups, tiles), out_shape=(jax.S...  47.8 us
    pallas_call x1, Pallas kernels, body(): pl.pallas_call(finish, out_shape=(jax.ShapeDtypeStruct((lev, cols), F32),...  1.66 us

profile of v1, /device:TPU:1, one launch (start us, length us, event | category | flops | bytes accessed | tf_op | source)
XLA Modules:
  0.0 50.2 jit_solution(17791781263152123132)
XLA Ops:
  0.6 0.0 copy-start
  0.6 47.8 %shard_map.131 = (f32[128,4096]{1,0:T(8,128)S(1)}, f32[64,2560]{1,0:T(8,128)S(1)}, f32[1,4096]{1,0:T(1,128)S(1)}) custom-call(f32[128,4096]{1,0:T(8,128)} %state_hbm.1, f32[128,128]{1,0:T(8,128)} %vco_hbm.1, f32[1,128]{1,0:T(1,128)} %bitcast.10, bf16[8,128,128]{2,1,0:T(8,128)(2,1)} %blocks_hbm.1, s32[4,1280]{1,0:T(4,128)} %bitcast.7, s32[4,1280]{1,0:T(4,128)} %bitcast.8, ...), custom_call_target="tpu_custom_call" | custom-call | tf_op jit(solution)/shard_map/pallas_call | solution.py:553
  48.5 0.0 copy-done
  48.5 1.7 %shard_map.132 = (f32[128,4096]{1,0:T(8,128)}, f32[64,2560]{1,0:T(8,128)}) custom-call(f32[128,4096]{1,0:T(8,128)S(1)} %get-tuple-element.5.pre, f32[64,2560]{1,0:T(8,128)S(1)} %get-tuple-element.6.height, f32[1,4096]{1,0:T(1,128)S(1)} %get-tuple-element.7.rows, f32[1,128]{1,0:T(1,128)S(1)} %bitcast.6), custom_call_target="tpu_custom_call" | custom-call | tf_op jit(solution)/shard_map/pallas_call | solution.py:629
Async XLA Ops:
  0.6 47.9 %copy-start = (f32[128]{0:T(128)S(1)}, f32[128]{0:T(128)}, u32[]{:S(2)}) copy-start(f32[128]{0:T(128)} %param.15) | copy-start | bytes 1540

commit v2 on v1

--- a/solution.py
+++ b/solution.py
@@ -12,6 +12,13 @@
 LANES = 128
 HALO = 8
 TIME_STEP = 0.5
+
+
+FAR_FIRST = True
+
+
+def hops(i, n):
+    return min(i, n - i)
 
 
 def kernel(
@@ -49,6 +56,7 @@
     idx_v,
     idx_s,
     coef,
+    inv,
     field,
     w0,
     w1,
@@ -90,15 +98,33 @@
     n_chunk = cols // chunk
     core, side = lax.rem(tile, 2), tiles // 2
     n_chip = groups * side
-    chip = group * side + lax.div(tile, 2)
     partner = tile + 1 - 2 * core
     half = n_flux // 2
     part_rows = side * nrows
     span = n_ocean + 2 * LANES
 
-    def chip_peer(i):
-        other = lax.rem(chip + i, n_chip)
-        return lax.div(other, side), 2 * lax.rem(other, side) + core
+    lane_of_chip = lax.div(tile, 2)
+    chip = group * side + lane_of_chip
+
+    def around(value, size):
+        return jnp.where(value >= size, value - size, value)
+
+    def far_first(n):
+        return sorted(range(n), key=lambda i: -min(i, n - i))
+
+    wide = 4 if side % 4 == 0 else 1
+    chip_order = [a * (side // wide) + b for a in far_first(wide) for b in far_first(side // wide)]
+    chip_order.sort(key=lambda q: -(hops(q // (side // wide), wide) + hops(q % (side // wide), side // wide)))
+    order = far_first(groups) if FAR_FIRST else far_first(groups)[::-1]
+
+    def chip_peer(dg, dq):
+        return around(group + dg, groups), 2 * around(lane_of_chip + dq, side) + core
+
+    def tile_peer(dt):
+        return group, around(tile + dt, tiles)
+
+    chip_offsets = [(dg, dq) for dg in order for dq in chip_order if dg or dq]
+    tile_offsets = [2 * dq + dc for dq in chip_order for dc in (0, 1) if dq or dc]
 
     loads = {
         name: pltpu.make_async_copy(source, target, load_sem.at[i])
@@ -117,32 +143,22 @@
             )
         )
     }
-    loads["vco"].start()
-
     def load_state(i):
         part = pl.ds(i * chunk, chunk)
         return pltpu.make_async_copy(state_hbm.at[:, part], state.at[:, part], in_sem.at[i])
 
+    loads["vco"].start()
+    loads["weight"].start()
     for i in range(n_chunk):
         load_state(i).start()
 
     barrier = pltpu.get_barrier_semaphore()
-
-    def greet(target):
+    for target in [chip_peer(*d) for d in chip_offsets] + [
+        (group, 2 * around(lane_of_chip + dq, side) + 1 - core) for dq in chip_order
+    ]:
         pl.semaphore_signal(barrier, inc=1, device_id=target, device_id_type=MESH)
-
-    def greet_chip(i, carry):
-        greet(chip_peer(i))
-        return carry
-
-    def greet_other_core(i, carry):
-        greet((group, 2 * i + 1 - core))
-        return carry
-
-    lax.fori_loop(1, n_chip, greet_chip, 0)
-    lax.fori_loop(0, side, greet_other_core, 0)
     for name in loads:
-        if name != "vco":
+        if name not in ("vco", "weight"):
             loads[name].start()
 
     loads["vco"].wait()
@@ -174,8 +190,10 @@
         for k in range(chunk // LANES):
             fluxf[i * (chunk // LANES) + k : i * (chunk // LANES) + k + 1, :] = line[:, k * LANES : (k + 1) * LANES]
 
-    for i in range(n_chunk - 1):
+    for i in range(n_chunk):
         first_steps(i)
+    mine = pl.ds(pl.multiple_of(core * half + chip * nrows, nrows), nrows)
+    flux_all[mine, :] = fluxf[...].astype(BF16)
 
     for name in ("mask", "depth", "source", "entry", "present", "wanted"):
         loads[name].wait()
@@ -195,15 +213,6 @@
 
     pl.semaphore_wait(barrier, n_chip - 1 + side)
 
-    start = lambda c: c.start()
-
-    def each(make, what, first, last):
-        def step(i, carry):
-            what(make(i))
-            return carry
-
-        lax.fori_loop(first, last, step, 0)
-
     def many(ref, rows, send_sem, recv_sem):
         return pltpu.make_async_remote_copy(
             src_ref=ref.at[pl.ds(0, rows)],
@@ -214,34 +223,32 @@
             device_id_type=MESH,
         )
 
-    def request(i):
+    def request(target):
         return pltpu.make_async_remote_copy(
             src_ref=req_v.at[own_slot],
             dst_ref=req_v.at[own_slot],
             send_sem=req_ssem,
             recv_sem=req_rsem,
-            device_id=(group, lax.rem(tile + i, tiles)),
+            device_id=target,
             device_id_type=MESH,
         )
 
-    each(request, start, 1, tiles)
+    for d in tile_offsets:
+        request(tile_peer(d)).start()
     requests = many(req_v, (tiles - 1) * 8, req_ssem, req_rsem)
 
-    first_steps(n_chunk - 1)
-    mine = pl.ds(pl.multiple_of(core * half + chip * nrows, nrows), nrows)
-    flux_all[mine, :] = fluxf[...].astype(BF16)
-
-    def flux_copy(i):
+    def flux_copy(target):
         return pltpu.make_async_remote_copy(
             src_ref=flux_all.at[mine],
             dst_ref=flux_all.at[mine],
             send_sem=flux_ssem,
             recv_sem=flux_rsem.at[group],
-            device_id=chip_peer(i),
+            device_id=target,
             device_id_type=MESH,
         )
 
-    each(flux_copy, start, 1, n_chip)
+    for d in chip_offsets:
+        flux_copy(chip_peer(*d)).start()
 
     after, before = lax.rem(tile + 1, tiles), lax.rem(tile + tiles - 1, tiles)
 
@@ -276,15 +283,14 @@
         s = state[:, part]
         pre[:, part] = s + tendency(s)
 
-    requests.wait_recv()
-    asked = jnp.concatenate([req_v[8 * t : 8 * t + 1, :] for t in range(tiles)], axis=0)
-    asked = jnp.concatenate([asked - tile * n_ocean, jnp.zeros((LANES - tiles, LANES), I32)], axis=0)
-    asked = jnp.transpose(asked)
-    where_col = lax.broadcasted_iota(I32, (nrows, n_ocean), 1)
-    stacked = lax.rem(where_col, own) * per + lax.div(where_col, own)
-    for t in range(tiles):
-        hit = asked[0:nrows, t : t + 1] == stacked
-        picks[t * nrows : (t + 1) * nrows, :] = jnp.where(hit, 1.0, 0.0).astype(BF16)
+    zero_rows = jnp.zeros((HALO, width), F32)
+    field[0:HALO, :] = zero_rows
+    field[HALO + own : ext, :] = zero_rows
+
+    def reciprocal(value):
+        return jnp.where(value > 0.0, 1.0 / jnp.where(value > 0.0, value, 1.0), 0.0)
+
+    inv[HALO : HALO + own, :] = reciprocal(coef[HALO : HALO + own, :])
 
     loads["blocks"].wait()
     pairs = [jnp.concatenate([blocks_ref[b], blocks_ref[b + 1]], axis=1) for b in range(0, n_block, 2)]
@@ -308,17 +314,16 @@
             device_id_type=MESH,
         )
 
-    order = [0] + [k for n in range(1, groups // 2 + 1) for k in sorted({n, groups - n})]
     for n, offset in enumerate(order):
-        g = lax.rem(group + offset, groups)
+        g = around(group + offset, groups)
         blocks_in = side - 1 if offset == 0 else side
         many(flux_all, blocks_in * nrows, flux_ssem, flux_rsem.at[g]).wait_recv()
         forward(g).start()
-        products(core * half + g * part_rows)
         if n > 0:
-            late = lax.rem(group + order[n - 1], groups)
+            late = around(group + order[n - 1], groups)
             forward(late).wait_recv()
             products((1 - core) * half + late * part_rows)
+        products(core * half + g * part_rows)
         if n == len(order) - 2:
             for copy in halos:
                 copy.wait()
@@ -330,25 +335,19 @@
             ]
             for copy in index_copies:
                 copy.start()
-            inner = jnp.where(coef[...] > 0.0, 1.0 / coef[...], 0.0)
-            coef[...] = inner
-            coef[0:HALO, :] = jnp.where(tile > 0, inner[0:HALO], 0.0)
-            coef[HALO + own : ext, :] = jnp.where(tile < tiles - 1, inner[HALO + own : ext], 0.0)
-            zero_rows = jnp.zeros((HALO, width), F32)
-            field[0:HALO, :] = zero_rows
-            field[HALO + own : ext, :] = zero_rows
-            for copy in index_copies:
-                copy.wait()
-    late = lax.rem(group + order[-1], groups)
+            inv[0:HALO, :] = jnp.where(tile > 0, reciprocal(coef[0:HALO, :]), 0.0)
+            inv[HALO + own : ext, :] = jnp.where(tile < tiles - 1, reciprocal(coef[HALO + own : ext, :]), 0.0)
+    late = around(group + order[-1], groups)
     forward(late).wait_recv()
     products((1 - core) * half + late * part_rows)
 
     def forcing_rows(g_tile, j, rows):
-        base = g_tile * 8 * per + j
+        first_row = g_tile * 8 * per + j + (rows[0] - HALO) * per + LANES
+        near = [idx_s.at[pl.ds(first_row + k * span, span)] for k in range(n_entry)]
         totals = []
         for s in rows:
-            e = base + ((s - HALO) * per + LANES)
-            got = [table[pl.ds(idx_s[e + k * span], 1), :] for k in range(n_entry)]
+            e = (s - rows[0]) * per
+            got = [table[pl.ds(near[k][e], 1), :] for k in range(n_entry)]
             while len(got) > 1:
                 got = [sum(got[k : k + 2][1:], got[k]) for k in range(0, len(got), 2)]
             totals.append(got[0])
@@ -362,6 +361,8 @@
         forcing_rows(ext // 8 - 1, j, (0, 1, 2))
         return carry
 
+    for copy in index_copies:
+        copy.wait()
     lax.fori_loop(0, per, edge, 0)
 
     def inside_rows(n, carry):
@@ -395,7 +396,7 @@
 
     def first(k, carry):
         f = rows8(field, k)
-        w = rows8(coef, k) * f
+        w = rows8(inv, k) * f
         w0[pl.ds(pl.multiple_of(k * 8, 8), 8), :] = w
         inside = jnp.logical_and(k >= 1, k < n_tile - 1)
         return carry + jnp.where(inside, folded(w * f), 0.0)
@@ -405,7 +406,7 @@
     def apply(w_old, w_new, k, carry):
         a, b = carry
         q = rows8(field, k) - beside(w_old, k)
-        w = rows8(coef, k) * q
+        w = rows8(inv, k) * q
         field[pl.ds(pl.multiple_of(k * 8, 8), 8), :] = q
         w_new[pl.ds(pl.multiple_of(k * 8, 8), 8), :] = w
         inside = jnp.logical_and(k >= 1, k < n_tile - 1)
@@ -428,17 +429,28 @@
     gram_slot = pl.ds(pl.multiple_of(tile * 8, 8), 8)
     gram_recv[gram_slot, :] = gram_send[...]
 
-    def gram_copy(i):
+    def gram_copy(target):
         return pltpu.make_async_remote_copy(
             src_ref=gram_send,
             dst_ref=gram_recv.at[gram_slot],
             send_sem=gram_ssem,
             recv_sem=gram_rsem,
-            device_id=(group, lax.rem(tile + i, tiles)),
+            device_id=target,
             device_id_type=MESH,
         )
 
-    each(gram_copy, start, 1, tiles)
+    for d in tile_offsets:
+        gram_copy(tile_peer(d)).start()
+    requests.wait_recv()
+    asked = jnp.concatenate([req_v[8 * t : 8 * t + 1, :] for t in range(tiles)], axis=0)
+    asked = jnp.concatenate([asked - tile * n_ocean, jnp.zeros((LANES - tiles, LANES), I32)], axis=0)
+    asked = jnp.transpose(asked)
+    where_col = lax.broadcasted_iota(I32, (nrows, n_ocean), 1)
+    stacked = lax.rem(where_col, own) * per + lax.div(where_col, own)
+    for t in range(tiles):
+        hit = asked[0:nrows, t : t + 1] == stacked
+        picks[t * nrows : (t + 1) * nrows, :] = jnp.where(hit, 1.0, 0.0).astype(BF16)
+
     gram_all = many(gram_recv, (tiles - 1) * 8, gram_ssem, gram_rsem)
     gram_all.wait_recv()
     total = jnp.sum(gram_recv[...].reshape(tiles, 8, LANES), axis=0)
@@ -477,20 +489,11 @@
     loads["temp"].wait()
     lax.fori_loop(0, own // 16, combine, 0)
 
-    n_req = tiles * nrows
-    at_once = min(256, n_req)
-
-    def picked(i, carry):
-        part = pl.ds(pl.multiple_of(i * at_once, at_once), at_once)
-        rows_send[part, :] = jnp.dot(picks[part, :], sst[...], preferred_element_type=F32).astype(BF16)
-        return carry
-
-    lax.fori_loop(0, n_req // at_once, picked, 0)
     rows_slot = pl.ds(pl.multiple_of(tile * nrows, nrows), nrows)
-    rows_recv[rows_slot, :] = rows_send[rows_slot, :]
-
-    def rows_copy(i):
-        other = lax.rem(tile + i, tiles)
+    wide_tiles = tiles // wide
+    plane = lax.div(tile, wide_tiles)
+
+    def rows_copy(other):
         return pltpu.make_async_remote_copy(
             src_ref=rows_send.at[pl.ds(pl.multiple_of(other * nrows, nrows), nrows)],
             dst_ref=rows_recv.at[rows_slot],
@@ -500,7 +503,15 @@
             device_id_type=MESH,
         )
 
-    each(rows_copy, start, 1, tiles)
+    within = lax.rem(tile, wide_tiles)
+    for dp in far_first(wide):
+        goal = around(plane + dp, wide) * wide_tiles
+        part = pl.ds(pl.multiple_of(goal * nrows, wide_tiles * nrows), wide_tiles * nrows)
+        rows_send[part, :] = jnp.dot(picks[part, :], sst[...], preferred_element_type=F32).astype(BF16)
+        for dt in far_first(wide_tiles):
+            if dp or dt:
+                rows_copy(goal + around(within + dt, wide_tiles)).start()
+    rows_recv[rows_slot, :] = rows_send[rows_slot, :]
     rows_all = many(rows_recv, (tiles - 1) * nrows, rows_ssem, rows_rsem)
     rows_all.wait_recv()
     got = jnp.sum(rows_recv[...].astype(F32).reshape(tiles, nrows, LANES), axis=0)
@@ -576,7 +587,8 @@
                 pltpu.VMEM((n_flux, LANES), BF16),
                 pltpu.VMEM((n_block * n_flux + 8, LANES), F32),
                 pltpu.VMEM((n_entry, 1, n_ocean + 2 * LANES), I32),
-                pltpu.SMEM((n_entry * (n_ocean + 2 * LANES),), I32),
+                pltpu.SMEM(((n_entry + 1) * (n_ocean + 2 * LANES),), I32),
+                pltpu.VMEM((ext, width), F32),
                 pltpu.VMEM((ext, width), F32),
                 pltpu.VMEM((ext, width), F32),
                 pltpu.VMEM((ext, width), F32),

time: 50.3 us -> 44.5 us (0.88)
  Pallas kernels: 49.5 us -> 43.7 us
    pallas_call x1, Pallas kernels: 47.8 us -> 42 us  [body(): pl.pallas_call(functools.partial(kernel, groups, tiles), out_shape=(jax.S...]
where the time goes in v2:
time: 44.5 us; the launch traced here: 44.3 us
  Pallas kernels  43.7 us (98%)
  between operations  0.66 us (1%)
    pallas_call x1, Pallas kernels, body(): pl.pallas_call(functools.partial(kernel, groups, tiles), out_shape=(jax.S...  42 us
    pallas_call x1, Pallas kernels, body(): pl.pallas_call(finish, out_shape=(jax.ShapeDtypeStruct((lev, cols), F32),...  1.66 us

profile of v2, /device:TPU:1, one launch (start us, length us, event | category | flops | bytes accessed | tf_op | source)
XLA Modules:
  0.0 44.3 jit_solution(15453668943844432288)
XLA Ops:
  0.6 0.0 copy-start
  0.6 42.0 %shard_map.131 = (f32[128,4096]{1,0:T(8,128)S(1)}, f32[64,2560]{1,0:T(8,128)S(1)}, f32[1,4096]{1,0:T(1,128)S(1)}) custom-call(f32[128,4096]{1,0:T(8,128)} %state_hbm.1, f32[128,128]{1,0:T(8,128)} %vco_hbm.1, f32[1,128]{1,0:T(1,128)} %bitcast.10, bf16[8,128,128]{2,1,0:T(8,128)(2,1)} %blocks_hbm.1, s32[4,1280]{1,0:T(4,128)} %bitcast.7, s32[4,1280]{1,0:T(4,128)} %bitcast.8, ...), custom_call_target="tpu_custom_call" | custom-call | tf_op jit(solution)/shard_map/pallas_call | solution.py:564
  42.7 0.0 copy-done
  42.7 1.7 %shard_map.132 = (f32[128,4096]{1,0:T(8,128)}, f32[64,2560]{1,0:T(8,128)}) custom-call(f32[128,4096]{1,0:T(8,128)S(1)} %get-tuple-element.5.pre, f32[64,2560]{1,0:T(8,128)S(1)} %get-tuple-element.6.height, f32[1,4096]{1,0:T(1,128)S(1)} %get-tuple-element.7.rows, f32[1,128]{1,0:T(1,128)S(1)} %bitcast.6), custom_call_target="tpu_custom_call" | custom-call | tf_op jit(solution)/shard_map/pallas_call | solution.py:641
Async XLA Ops:
  0.6 42.0 %copy-start = (f32[128]{0:T(128)S(1)}, f32[128]{0:T(128)}, u32[]{:S(2)}) copy-start(f32[128]{0:T(128)} %param.15) | copy-start | bytes 1540

commit v3 on v2

--- a/solution.py
+++ b/solution.py
@@ -35,9 +35,11 @@
     depth_hbm,
     temp_hbm,
     wanted_hbm,
+    response_hbm,
     pre,
     height,
     rows_out,
+    column_out,
     state,
     vco_ref,
     weight_ref,
@@ -49,6 +51,7 @@
     depth_ref,
     temp_ref,
     wanted_ref,
+    response_ref,
     vv,
     fluxf,
     flux_all,
@@ -140,23 +143,28 @@
                 ("wanted", wanted_hbm, wanted_ref),
                 ("blocks", blocks_hbm, blocks_ref),
                 ("temp", temp_hbm, temp_ref),
+                ("response", response_hbm, response_ref),
             )
         )
     }
+
     def load_state(i):
         part = pl.ds(i * chunk, chunk)
         return pltpu.make_async_copy(state_hbm.at[:, part], state.at[:, part], in_sem.at[i])
 
+    barrier = pltpu.get_barrier_semaphore()
+    greeted = [chip_peer(*d) for d in chip_offsets]
+    greeted += [(group, 2 * around(lane_of_chip + dq, side) + 1 - core) for dq in chip_order]
+
+    def greet(targets):
+        for target in targets:
+            pl.semaphore_signal(barrier, inc=1, device_id=target, device_id_type=MESH)
+
     loads["vco"].start()
-    loads["weight"].start()
     for i in range(n_chunk):
         load_state(i).start()
-
-    barrier = pltpu.get_barrier_semaphore()
-    for target in [chip_peer(*d) for d in chip_offsets] + [
-        (group, 2 * around(lane_of_chip + dq, side) + 1 - core) for dq in chip_order
-    ]:
-        pl.semaphore_signal(barrier, inc=1, device_id=target, device_id_type=MESH)
+    greet(greeted)
+    loads["weight"].start()
     for name in loads:
         if name not in ("vco", "weight"):
             loads[name].start()
@@ -176,24 +184,48 @@
         both = jnp.dot(vv[...], jnp.concatenate([hi, lo], axis=0), preferred_element_type=F32)
         return TIME_STEP * jnp.tanh(both[0:lev] + both[lev : 2 * lev])
 
+    for i in range(n_chunk):
+        load_state(i).wait()
     loads["weight"].wait()
     column = jnp.transpose(jnp.broadcast_to(weight_ref[...], (LANES, lev)))[:, 0:1]
-
-    def first_steps(i):
-        load_state(i).wait()
-        part = pl.ds(i * chunk, chunk)
+    parts = [pl.ds(i * chunk, chunk) for i in range(n_chunk)]
+    for part in parts:
         s = state[:, part]
-        s = s + tendency(s)
+        state[:, part] = s + tendency(s)
+    for i, part in enumerate(parts):
+        s = state[:, part]
         s = s + tendency(s)
         state[:, part] = s
         line = jnp.sum(s * column, axis=0, keepdims=True)
         for k in range(chunk // LANES):
             fluxf[i * (chunk // LANES) + k : i * (chunk // LANES) + k + 1, :] = line[:, k * LANES : (k + 1) * LANES]
-
-    for i in range(n_chunk):
-        first_steps(i)
     mine = pl.ds(pl.multiple_of(core * half + chip * nrows, nrows), nrows)
     flux_all[mine, :] = fluxf[...].astype(BF16)
+
+    pl.semaphore_wait(barrier, n_chip - 1 + side)
+
+    def many(ref, rows, send_sem, recv_sem):
+        return pltpu.make_async_remote_copy(
+            src_ref=ref.at[pl.ds(0, rows)],
+            dst_ref=ref.at[pl.ds(0, rows)],
+            send_sem=send_sem,
+            recv_sem=recv_sem,
+            device_id=(group, partner),
+            device_id_type=MESH,
+        )
+
+    def flux_copy(target):
+        return pltpu.make_async_remote_copy(
+            src_ref=flux_all.at[mine],
+            dst_ref=flux_all.at[mine],
+            send_sem=flux_ssem,
+            recv_sem=flux_rsem.at[group],
+            device_id=target,
+            device_id_type=MESH,
+        )
+
+    for d in chip_offsets:
+        flux_copy(chip_peer(*d)).start()
 
     for name in ("mask", "depth", "source", "entry", "present", "wanted"):
         loads[name].wait()
@@ -211,18 +243,6 @@
     req_v[own_slot, 0:nrows] = jnp.broadcast_to(wanted_ref[...], (8, nrows))
     table[pl.ds(spare, 8), :] = jnp.zeros((8, LANES), F32)
 
-    pl.semaphore_wait(barrier, n_chip - 1 + side)
-
-    def many(ref, rows, send_sem, recv_sem):
-        return pltpu.make_async_remote_copy(
-            src_ref=ref.at[pl.ds(0, rows)],
-            dst_ref=ref.at[pl.ds(0, rows)],
-            send_sem=send_sem,
-            recv_sem=recv_sem,
-            device_id=(group, partner),
-            device_id_type=MESH,
-        )
-
     def request(target):
         return pltpu.make_async_remote_copy(
             src_ref=req_v.at[own_slot],
@@ -236,19 +256,6 @@
     for d in tile_offsets:
         request(tile_peer(d)).start()
     requests = many(req_v, (tiles - 1) * 8, req_ssem, req_rsem)
-
-    def flux_copy(target):
-        return pltpu.make_async_remote_copy(
-            src_ref=flux_all.at[mine],
-            dst_ref=flux_all.at[mine],
-            send_sem=flux_ssem,
-            recv_sem=flux_rsem.at[group],
-            device_id=target,
-            device_id_type=MESH,
-        )
-
-    for d in chip_offsets:
-        flux_copy(chip_peer(*d)).start()
 
     after, before = lax.rem(tile + 1, tiles), lax.rem(tile + tiles - 1, tiles)
 
@@ -283,14 +290,22 @@
         s = state[:, part]
         pre[:, part] = s + tendency(s)
 
-    zero_rows = jnp.zeros((HALO, width), F32)
-    field[0:HALO, :] = zero_rows
-    field[HALO + own : ext, :] = zero_rows
+    loads["response"].wait()
+    column_out[...] = TIME_STEP * jnp.transpose(jnp.broadcast_to(response_ref[...], (LANES, lev)))
+
+    zero_rows = jnp.zeros((per, HALO, LANES), F32)
+    field[:, 0:HALO, :] = zero_rows
+    field[:, HALO + own : ext, :] = zero_rows
 
     def reciprocal(value):
         return jnp.where(value > 0.0, 1.0 / jnp.where(value > 0.0, value, 1.0), 0.0)
 
-    inv[HALO : HALO + own, :] = reciprocal(coef[HALO : HALO + own, :])
+    def set_inverse(first, last, exists):
+        for j in range(per):
+            value = reciprocal(coef[first:last, j * LANES : (j + 1) * LANES])
+            inv[j, first:last, :] = value if exists is None else jnp.where(exists, value, 0.0)
+
+    set_inverse(HALO, HALO + own, None)
 
     loads["blocks"].wait()
     pairs = [jnp.concatenate([blocks_ref[b], blocks_ref[b + 1]], axis=1) for b in range(0, n_block, 2)]
@@ -314,45 +329,58 @@
             device_id_type=MESH,
         )
 
-    for n, offset in enumerate(order):
+    def take(offset):
         g = around(group + offset, groups)
         blocks_in = side - 1 if offset == 0 else side
         many(flux_all, blocks_in * nrows, flux_ssem, flux_rsem.at[g]).wait_recv()
         forward(g).start()
-        if n > 0:
-            late = around(group + order[n - 1], groups)
-            forward(late).wait_recv()
-            products((1 - core) * half + late * part_rows)
-        products(core * half + g * part_rows)
-        if n == len(order) - 2:
-            for copy in halos:
-                copy.wait()
-            index_copies = [
-                pltpu.make_async_copy(
-                    idx_v.at[k, 0], idx_s.at[pl.ds(k * span, span)], idx_sem.at[k]
-                )
-                for k in range(n_entry)
-            ]
-            for copy in index_copies:
-                copy.start()
-            inv[0:HALO, :] = jnp.where(tile > 0, reciprocal(coef[0:HALO, :]), 0.0)
-            inv[HALO + own : ext, :] = jnp.where(tile < tiles - 1, reciprocal(coef[HALO + own : ext, :]), 0.0)
-    late = around(group + order[-1], groups)
-    forward(late).wait_recv()
-    products((1 - core) * half + late * part_rows)
+
+    def near(offset):
+        products(core * half + around(group + offset, groups) * part_rows)
+
+    def far(offset):
+        products((1 - core) * half + around(group + offset, groups) * part_rows)
+
+    def shared(offset):
+        forward(around(group + offset, groups)).wait_recv()
+
+    take(order[0])
+    near(order[0])
+    take(order[1])
+    shared(order[0])
+    near(order[1])
+    far(order[0])
+    for offset in order[2:]:
+        take(offset)
+    shared(order[1])
+    for offset in order[2:]:
+        near(offset)
+    far(order[1])
+    for copy in halos:
+        copy.wait()
+    index_copies = [
+        pltpu.make_async_copy(idx_v.at[k, 0], idx_s.at[pl.ds(k * span, span)], idx_sem.at[k]) for k in range(n_entry)
+    ]
+    for copy in index_copies:
+        copy.start()
+    set_inverse(0, HALO, tile > 0)
+    set_inverse(HALO + own, ext, tile < tiles - 1)
+    for offset in order[2:]:
+        shared(offset)
+    for offset in order[2:]:
+        far(offset)
 
     def forcing_rows(g_tile, j, rows):
         first_row = g_tile * 8 * per + j + (rows[0] - HALO) * per + LANES
-        near = [idx_s.at[pl.ds(first_row + k * span, span)] for k in range(n_entry)]
         totals = []
         for s in rows:
-            e = (s - rows[0]) * per
-            got = [table[pl.ds(near[k][e], 1), :] for k in range(n_entry)]
+            e = first_row + (s - rows[0]) * per
+            got = [table[pl.ds(idx_s.at[pl.ds(e + k * span, 1)][0], 1), :] for k in range(n_entry)]
             while len(got) > 1:
                 got = [sum(got[k : k + 2][1:], got[k]) for k in range(0, len(got), 2)]
             totals.append(got[0])
         at = pl.multiple_of(g_tile * 8, 8)
-        block = field.at[pl.ds(at, 8), pl.ds(pl.multiple_of(j * LANES, LANES), LANES)]
+        block = field.at[j, pl.ds(at, 8), :]
         for s, total in zip(rows, totals):
             block[s : s + 1, :] = total
 
@@ -365,63 +393,58 @@
         copy.wait()
     lax.fori_loop(0, per, edge, 0)
 
-    def inside_rows(n, carry):
-        forcing_rows(1 + lax.div(n, per), lax.rem(n, per), range(8))
-        return carry
-
-    lax.fori_loop(0, own // 8 * per, inside_rows, 0, unroll=2)
+    def inside_rows(g_tile, carry):
+        def one(j, inner):
+            forcing_rows(g_tile, j, range(8))
+            return inner
+
+        return lax.fori_loop(0, per, one, carry, unroll=5)
+
+    lax.fori_loop(1, 1 + own // 8, inside_rows, 0)
 
     n_tile = ext // 8
-    top = lax.broadcasted_iota(I32, (8, width), 0) == 0
-    bottom = lax.broadcasted_iota(I32, (8, width), 0) == 7
+    lane = lax.broadcasted_iota(I32, (per, 8, LANES), 2)
 
     def rows8(ref, k):
-        return ref[pl.ds(pl.multiple_of(k * 8, 8), 8), :]
+        return ref[:, 8 * k : 8 * k + 8, :]
 
     def beside(ref, k):
         here = rows8(ref, k)
-        above = rows8(ref, jnp.maximum(k - 1, 0))
-        below = rows8(ref, jnp.minimum(k + 1, n_tile - 1))
-        up = jnp.where(top, pltpu.roll(above, 1, 0), pltpu.roll(here, 1, 0))
-        down = jnp.where(bottom, pltpu.roll(below, 7, 0), pltpu.roll(here, 7, 0))
-        return up + down + pltpu.roll(here, 1, 1) + pltpu.roll(here, width - 1, 1)
-
-    def folded(value):
-        total = value[:, 0:LANES]
-        for k in range(1, per):
-            total = total + value[:, k * LANES : (k + 1) * LANES]
-        return total
+        up = ref[:, 8 * k - 1 : 8 * k + 7, :] if k > 0 else pltpu.roll(here, 1, 1)
+        down = ref[:, 8 * k + 1 : 8 * k + 9, :] if k < n_tile - 1 else pltpu.roll(here, 7, 1)
+        one, other = pltpu.roll(here, 1, 2), pltpu.roll(here, LANES - 1, 2)
+        left = jnp.where(lane == 0, jnp.concatenate([one[per - 1 :], one[: per - 1]], axis=0), one)
+        right = jnp.where(lane == LANES - 1, jnp.concatenate([other[1:], other[:1]], axis=0), other)
+        return (up + down) + (left + right)
 
     nothing = jnp.zeros((8, LANES), F32)
-
-    def first(k, carry):
+    own_tiles = range(1, n_tile - 1)
+
+    nu0 = nothing
+    for k in range(n_tile):
         f = rows8(field, k)
         w = rows8(inv, k) * f
-        w0[pl.ds(pl.multiple_of(k * 8, 8), 8), :] = w
-        inside = jnp.logical_and(k >= 1, k < n_tile - 1)
-        return carry + jnp.where(inside, folded(w * f), 0.0)
-
-    nu0 = lax.fori_loop(0, n_tile, first, nothing, unroll=5)
-
-    def apply(w_old, w_new, k, carry):
-        a, b = carry
-        q = rows8(field, k) - beside(w_old, k)
-        w = rows8(inv, k) * q
-        field[pl.ds(pl.multiple_of(k * 8, 8), 8), :] = q
-        w_new[pl.ds(pl.multiple_of(k * 8, 8), 8), :] = w
-        inside = jnp.logical_and(k >= 1, k < n_tile - 1)
-        a = a + jnp.where(inside, folded(rows8(w_old, k) * q), 0.0)
-        b = b + jnp.where(inside, folded(w * q), 0.0)
+        w0[:, 8 * k : 8 * k + 8, :] = w
+        if k in own_tiles:
+            nu0 = nu0 + jnp.sum(w * f, axis=0)
+
+    def apply(w_old, w_new):
+        a, b = nothing, nothing
+        for k in range(n_tile):
+            q = rows8(field, k) - beside(w_old, k)
+            w = rows8(inv, k) * q
+            field[:, 8 * k : 8 * k + 8, :] = q
+            w_new[:, 8 * k : 8 * k + 8, :] = w
+            if k in own_tiles:
+                a = a + jnp.sum(rows8(w_old, k) * q, axis=0)
+                b = b + jnp.sum(w * q, axis=0)
         return a, b
 
-    nu1, nu2 = lax.fori_loop(0, n_tile, functools.partial(apply, w0, w1), (nothing, nothing), unroll=5)
-    nu3, nu4 = lax.fori_loop(0, n_tile, functools.partial(apply, w1, w2), (nothing, nothing), unroll=5)
-
-    def last(k, carry):
-        q = rows8(field, k) - beside(w2, k)
-        return carry + folded(rows8(w2, k) * q)
-
-    nu5 = lax.fori_loop(1, n_tile - 1, last, nothing, unroll=4)
+    nu1, nu2 = apply(w0, w1)
+    nu3, nu4 = apply(w1, w2)
+    nu5 = nothing
+    for k in own_tiles:
+        nu5 = nu5 + jnp.sum(rows8(w2, k) * (rows8(field, k) - beside(w2, k)), axis=0)
 
     gram_send[...] = jnp.zeros((8, LANES), F32)
     for k, nu in enumerate((nu0, nu1, nu2, nu3, nu4, nu5)):
@@ -473,21 +496,14 @@
     c2 = y2 * i2
     c1 = y1 * i1 - l3 * c2
     c0 = n0 * i0 - l1 * c1 - l2 * c2
-    c0, c1, c2 = (jnp.broadcast_to(c, (1, width)) for c in (c0, c1, c2))
-
-    def combine(k, carry):
-        at = pl.multiple_of(k * 16, 16)
-        inner_at = pl.multiple_of(HALO + k * 16, 8)
-        part = pl.ds(inner_at, 16)
-        x = c0 * w0[part, :] + c1 * w1[part, :] + c2 * w2[part, :]
-        height[pl.ds(at, 16), :] = x
-        warm = jnp.where(mask_ref[pl.ds(at, 16), :] == 1, temp_ref[pl.ds(at, 16), :] + x, 0.0).astype(BF16)
-        for j in range(per):
-            sst[pl.ds(pl.multiple_of(j * own + k * 16, 16), 16), :] = warm[:, j * LANES : (j + 1) * LANES]
-        return carry
+    c0, c1, c2 = (jnp.broadcast_to(c, (1, LANES)) for c in (c0, c1, c2))
 
     loads["temp"].wait()
-    lax.fori_loop(0, own // 16, combine, 0)
+    for j in range(per):
+        part = slice(j * LANES, (j + 1) * LANES)
+        x = c0 * w0[j, HALO : HALO + own, :] + c1 * w1[j, HALO : HALO + own, :] + c2 * w2[j, HALO : HALO + own, :]
+        height[:, part] = x
+        sst[j * own : (j + 1) * own, :] = jnp.where(mask_ref[:, part] == 1, temp_ref[:, part] + x, 0.0).astype(BF16)
 
     rows_slot = pl.ds(pl.multiple_of(tile * nrows, nrows), nrows)
     wide_tiles = tiles // wide
@@ -526,17 +542,17 @@
     rows_all.wait_send()
 
 
-def finish(pre, height, rows, response, atm_hbm, height_hbm, held, sems, height_sem):
+def finish(pre, height, rows, column, atm_hbm, height_hbm, held, sems, height_sem):
     copy = pltpu.make_async_copy(height, height_hbm, height_sem)
     copy.start()
     lev, cols = pre.shape
-    column = TIME_STEP * jnp.transpose(jnp.broadcast_to(response[...], (LANES, lev)))[:, 0:1]
     n_part = sems.shape[0]
     size = cols // n_part
     outs = []
     for i in range(n_part):
         part = pl.ds(i * size, size)
-        held[:, part] = pre[:, part] + column * rows[:, part]
+        for j in range(i * size, (i + 1) * size, LANES):
+            held[:, j : j + LANES] = pre[:, j : j + LANES] + column[...] * rows[:, j : j + LANES]
         outs.append(pltpu.make_async_copy(held.at[:, part], atm_hbm.at[:, part], sems.at[i]))
         outs[-1].start()
     for out in outs:
@@ -561,15 +577,16 @@
         n_block, n_entry = blocks.shape[0], source.shape[1]
         anywhere = pl.BlockSpec(memory_space=pltpu.HBM)
         dma = pltpu.SemaphoreType.DMA
-        pre, height, rows = pl.pallas_call(
+        pre, height, rows, column = pl.pallas_call(
             functools.partial(kernel, groups, tiles),
             out_shape=(
                 jax.ShapeDtypeStruct((lev, cols), F32),
                 jax.ShapeDtypeStruct((own, width), F32),
                 jax.ShapeDtypeStruct((1, cols), F32),
+                jax.ShapeDtypeStruct((lev, LANES), F32),
             ),
-            in_specs=[anywhere] * 11,
-            out_specs=(vmem, vmem, vmem),
+            in_specs=[anywhere] * 12,
+            out_specs=(vmem, vmem, vmem, vmem),
             scratch_shapes=[
                 pltpu.VMEM((lev, cols), F32),
                 pltpu.VMEM((lev, lev), F32),
@@ -582,6 +599,7 @@
                 pltpu.VMEM((own, width), F32),
                 pltpu.VMEM((own, width), F32),
                 pltpu.VMEM((1, nrows), I32),
+                pltpu.VMEM((1, lev), F32),
                 pltpu.VMEM((2 * lev, 2 * lev), BF16),
                 pltpu.VMEM((nrows, LANES), F32),
                 pltpu.VMEM((n_flux, LANES), BF16),
@@ -589,11 +607,11 @@
                 pltpu.VMEM((n_entry, 1, n_ocean + 2 * LANES), I32),
                 pltpu.SMEM(((n_entry + 1) * (n_ocean + 2 * LANES),), I32),
                 pltpu.VMEM((ext, width), F32),
-                pltpu.VMEM((ext, width), F32),
-                pltpu.VMEM((ext, width), F32),
-                pltpu.VMEM((ext, width), F32),
-                pltpu.VMEM((ext, width), F32),
-                pltpu.VMEM((ext, width), F32),
+                pltpu.VMEM((width // LANES, ext, LANES), F32),
+                pltpu.VMEM((width // LANES, ext, LANES), F32),
+                pltpu.VMEM((width // LANES, ext, LANES), F32),
+                pltpu.VMEM((width // LANES, ext, LANES), F32),
+                pltpu.VMEM((width // LANES, ext, LANES), F32),
                 pltpu.VMEM((tiles * 8, LANES), I32),
                 pltpu.VMEM((n_req, n_ocean), BF16),
                 pltpu.VMEM((n_ocean, LANES), BF16),
@@ -602,7 +620,7 @@
                 pltpu.VMEM((8, LANES), F32),
                 pltpu.VMEM((tiles * 8, LANES), F32),
                 dma((n_chunk,)),
-                dma((10,)),
+                dma((11,)),
                 dma((n_entry,)),
                 dma,
                 dma((groups,)),
@@ -635,6 +653,7 @@
                     depth,
                     temp,
                     wanted[None, :],
+                    response[None, :],
                 )
             )
         )
@@ -645,7 +664,7 @@
             out_specs=(anywhere, anywhere),
             scratch_shapes=[pltpu.VMEM((lev, cols), F32), dma((n_chunk,)), dma],
             compiler_params=pltpu.CompilerParams(vmem_limit_bytes=16 * 1024 * 1024),
-        )(pre, height, rows, response[None, :])
+        )(pre, height, rows, column)
 
     split = P(None, ("comp", "tile"))
     ocean = P("tile", None)

time: 44.5 us -> 41.4 us (0.930)
  Pallas kernels: 43.7 us -> 40.6 us
    pallas_call x1, Pallas kernels: 42 us -> 39.1 us  [body(): pl.pallas_call(functools.partial(kernel, groups, tiles), out_shape=(jax.S...]
where the time goes in v3:
time: 41.4 us; the launch traced here: 41.3 us
  Pallas kernels  40.6 us (98%)
  between operations  0.64 us (2%)
    pallas_call x1, Pallas kernels, body(): pl.pallas_call(functools.partial(kernel, groups, tiles), out_shape=(jax.S...  39.1 us
    pallas_call x1, Pallas kernels, body(): pl.pallas_call(finish, out_shape=(jax.ShapeDtypeStruct((lev, cols), F32),...  1.57 us

profile of v3, /device:TPU:1, one launch (start us, length us, event | category | flops | bytes accessed | tf_op | source)
XLA Modules:
  0.0 41.3 jit_solution(1166684396392878140)
XLA Ops:
  0.6 39.1 %shard_map.131 = (f32[128,4096]{1,0:T(8,128)S(1)}, f32[64,2560]{1,0:T(8,128)S(1)}, f32[1,4096]{1,0:T(1,128)S(1)}, f32[128,128]{1,0:T(8,128)S(1)}) custom-call(f32[128,4096]{1,0:T(8,128)} %state_hbm.1, f32[128,128]{1,0:T(8,128)} %vco_hbm.1, f32[1,128]{1,0:T(1,128)} %bitcast.9, bf16[8,128,128]{2,1,0:T(8,128)(2,1)} %blocks_hbm.1, s32[4,1280]{1,0:T(4,128)} %bitcast.6, ...), custom_call_target="tpu_custom_call" | custom-call | tf_op jit(solution)/shard_map/pallas_call | solution.py:580
  39.7 1.6 %shard_map.132 = (f32[128,4096]{1,0:T(8,128)}, f32[64,2560]{1,0:T(8,128)}) custom-call(f32[128,4096]{1,0:T(8,128)S(1)} %get-tuple-element.6.pre, f32[64,2560]{1,0:T(8,128)S(1)} %get-tuple-element.7.height, f32[1,4096]{1,0:T(1,128)S(1)} %get-tuple-element.8.rows, f32[128,128]{1,0:T(8,128)S(1)} %get-tuple-element.9.column), custom_call_target="tpu_custom_call" | custom-call | tf_op jit(solution)/shard_map/pallas_call | solution.py:660

commit v4 on v3

--- a/solution.py
+++ b/solution.py
@@ -202,6 +202,17 @@
     mine = pl.ds(pl.multiple_of(core * half + chip * nrows, nrows), nrows)
     flux_all[mine, :] = fluxf[...].astype(BF16)
 
+    for name in ("source", "entry", "present"):
+        loads[name].wait()
+    spare = n_block * n_flux
+    source = source_ref[...]
+    holder = lax.div(source, nrows)
+    row = lax.rem(holder, 2) * half + lax.div(holder, 2) * nrows + lax.rem(source, nrows)
+    index = jnp.where(present_ref[...] == 1, entry_ref[...] * n_flux + row, jnp.full(source.shape, spare, I32))
+    for k in range(n_entry):
+        idx_v[k, :, LANES : LANES + n_ocean] = index[k : k + 1, :]
+    table[pl.ds(spare, 8), :] = jnp.zeros((8, LANES), F32)
+
     pl.semaphore_wait(barrier, n_chip - 1 + side)
 
     def many(ref, rows, send_sem, recv_sem):
@@ -213,49 +224,6 @@
             device_id=(group, partner),
             device_id_type=MESH,
         )
-
-    def flux_copy(target):
-        return pltpu.make_async_remote_copy(
-            src_ref=flux_all.at[mine],
-            dst_ref=flux_all.at[mine],
-            send_sem=flux_ssem,
-            recv_sem=flux_rsem.at[group],
-            device_id=target,
-            device_id_type=MESH,
-        )
-
-    for d in chip_offsets:
-        flux_copy(chip_peer(*d)).start()
-
-    for name in ("mask", "depth", "source", "entry", "present", "wanted"):
-        loads[name].wait()
-    mask = mask_ref[...].astype(F32)
-    coef[HALO : HALO + own, :] = mask * (4.0 + depth_ref[...])
-    spare = n_block * n_flux
-    source = source_ref[...]
-    holder = lax.div(source, nrows)
-    row = lax.rem(holder, 2) * half + lax.div(holder, 2) * nrows + lax.rem(source, nrows)
-    index = jnp.where(present_ref[...] == 1, entry_ref[...] * n_flux + row, jnp.full(source.shape, spare, I32))
-    for k in range(n_entry):
-        idx_v[k, :, LANES : LANES + n_ocean] = index[k : k + 1, :]
-    own_slot = pl.ds(pl.multiple_of(tile * 8, 8), 8)
-    req_v[own_slot, :] = jnp.full((8, LANES), -1, I32)
-    req_v[own_slot, 0:nrows] = jnp.broadcast_to(wanted_ref[...], (8, nrows))
-    table[pl.ds(spare, 8), :] = jnp.zeros((8, LANES), F32)
-
-    def request(target):
-        return pltpu.make_async_remote_copy(
-            src_ref=req_v.at[own_slot],
-            dst_ref=req_v.at[own_slot],
-            send_sem=req_ssem,
-            recv_sem=req_rsem,
-            device_id=target,
-            device_id_type=MESH,
-        )
-
-    for d in tile_offsets:
-        request(tile_peer(d)).start()
-    requests = many(req_v, (tiles - 1) * 8, req_ssem, req_rsem)
 
     after, before = lax.rem(tile + 1, tiles), lax.rem(tile + tiles - 1, tiles)
 
@@ -282,7 +250,44 @@
             before,
         ),
     )
-    for copy in halos:
+    for copy in halos[2:]:
+        copy.start()
+
+    def flux_copy(target):
+        return pltpu.make_async_remote_copy(
+            src_ref=flux_all.at[mine],
+            dst_ref=flux_all.at[mine],
+            send_sem=flux_ssem,
+            recv_sem=flux_rsem.at[group],
+            device_id=target,
+            device_id_type=MESH,
+        )
+
+    for d in chip_offsets:
+        flux_copy(chip_peer(*d)).start()
+
+    for name in ("mask", "depth", "wanted"):
+        loads[name].wait()
+    coef[HALO : HALO + own, :] = mask_ref[...].astype(F32) * (4.0 + depth_ref[...])
+    own_slot = pl.ds(pl.multiple_of(tile * 8, 8), 8)
+    req_v[own_slot, :] = jnp.full((8, LANES), -1, I32)
+    req_v[own_slot, 0:nrows] = jnp.broadcast_to(wanted_ref[...], (8, nrows))
+
+    def request(target):
+        return pltpu.make_async_remote_copy(
+            src_ref=req_v.at[own_slot],
+            dst_ref=req_v.at[own_slot],
+            send_sem=req_ssem,
+            recv_sem=req_rsem,
+            device_id=target,
+            device_id_type=MESH,
+        )
+
+    for d in tile_offsets:
+        request(tile_peer(d)).start()
+    requests = many(req_v, (tiles - 1) * 8, req_ssem, req_rsem)
+
+    for copy in halos[:2]:
         copy.start()
 
     for i in range(n_chunk):
@@ -344,31 +349,53 @@
     def shared(offset):
         forward(around(group + offset, groups)).wait_recv()
 
-    take(order[0])
-    near(order[0])
-    take(order[1])
-    shared(order[0])
-    near(order[1])
-    far(order[0])
-    for offset in order[2:]:
-        take(offset)
-    shared(order[1])
-    for offset in order[2:]:
-        near(offset)
-    far(order[1])
-    for copy in halos:
+    ahead, behind = order[: len(order) // 2], order[len(order) // 2 :]
+
+    @pl.when(core == 1)
+    def _():
+        for offset in ahead:
+            take(offset)
+            near(offset)
+        for offset in behind:
+            take(offset)
+        for offset in behind:
+            near(offset)
+
+    @pl.when(core == 0)
+    def _():
+        for offset in ahead:
+            shared(offset)
+            far(offset)
+        for offset in ahead:
+            take(offset)
+        for offset in ahead:
+            near(offset)
+        for offset in behind:
+            take(offset)
+
+    for copy in halos[2:]:
         copy.wait()
     index_copies = [
         pltpu.make_async_copy(idx_v.at[k, 0], idx_s.at[pl.ds(k * span, span)], idx_sem.at[k]) for k in range(n_entry)
     ]
     for copy in index_copies:
         copy.start()
-    set_inverse(0, HALO, tile > 0)
-    set_inverse(HALO + own, ext, tile < tiles - 1)
-    for offset in order[2:]:
-        shared(offset)
-    for offset in order[2:]:
-        far(offset)
+
+    @pl.when(core == 1)
+    def _():
+        for some in (ahead, behind):
+            for offset in some:
+                shared(offset)
+            for offset in some:
+                far(offset)
+
+    @pl.when(core == 0)
+    def _():
+        for offset in behind:
+            shared(offset)
+        for offset in behind:
+            far(offset)
+            near(offset)
 
     def forcing_rows(g_tile, j, rows):
         first_row = g_tile * 8 * per + j + (rows[0] - HALO) * per + LANES
@@ -401,6 +428,11 @@
         return lax.fori_loop(0, per, one, carry, unroll=5)
 
     lax.fori_loop(1, 1 + own // 8, inside_rows, 0)
+
+    for copy in halos[:2]:
+        copy.wait()
+    set_inverse(0, HALO, tile > 0)
+    set_inverse(HALO + own, ext, tile < tiles - 1)
 
     n_tile = ext // 8
     lane = lax.broadcasted_iota(I32, (per, 8, LANES), 2)

time: 41.4 us -> 40.8 us (0.986)
  Pallas kernels: 40.6 us -> 40 us
    pallas_call x1, Pallas kernels: 39.1 us -> 38.4 us  [body(): pl.pallas_call(functools.partial(kernel, groups, tiles), out_shape=(jax.S...]
where the time goes in v4:
time: 40.8 us; the launch traced here: 40.6 us
  Pallas kernels  40 us (98%)
  between operations  0.64 us (2%)
    pallas_call x1, Pallas kernels, body(): pl.pallas_call(functools.partial(kernel, groups, tiles), out_shape=(jax.S...  38.4 us
    pallas_call x1, Pallas kernels, body(): pl.pallas_call(finish, out_shape=(jax.ShapeDtypeStruct((lev, cols), F32),...  1.57 us

profile of v4, /device:TPU:1, one launch (start us, length us, event | category | flops | bytes accessed | tf_op | source)
XLA Modules:
  0.0 40.6 jit_solution(3903529446067583650)
XLA Ops:
  0.6 38.4 %shard_map.131 = (f32[128,4096]{1,0:T(8,128)S(1)}, f32[64,2560]{1,0:T(8,128)S(1)}, f32[1,4096]{1,0:T(1,128)S(1)}, f32[128,128]{1,0:T(8,128)S(1)}) custom-call(f32[128,4096]{1,0:T(8,128)} %state_hbm.1, f32[128,128]{1,0:T(8,128)} %vco_hbm.1, f32[1,128]{1,0:T(1,128)} %bitcast.9, bf16[8,128,128]{2,1,0:T(8,128)(2,1)} %blocks_hbm.1, s32[4,1280]{1,0:T(4,128)} %bitcast.6, ...), custom_call_target="tpu_custom_call" | custom-call | tf_op jit(solution)/shard_map/pallas_call | solution.py:612
  39.1 1.6 %shard_map.132 = (f32[128,4096]{1,0:T(8,128)}, f32[64,2560]{1,0:T(8,128)}) custom-call(f32[128,4096]{1,0:T(8,128)S(1)} %get-tuple-element.6.pre, f32[64,2560]{1,0:T(8,128)S(1)} %get-tuple-element.7.height, f32[1,4096]{1,0:T(1,128)S(1)} %get-tuple-element.8.rows, f32[128,128]{1,0:T(8,128)S(1)} %get-tuple-element.9.column), custom_call_target="tpu_custom_call" | custom-call | tf_op jit(solution)/shard_map/pallas_call | solution.py:692

commit v5 on v4

--- a/solution.py
+++ b/solution.py
@@ -127,6 +127,13 @@
         return group, around(tile + dt, tiles)
 
     chip_offsets = [(dg, dq) for dg in order for dq in chip_order if dg or dq]
+    across = side // wide
+
+    def distance(offset):
+        dg, dq = offset
+        return hops(dg, groups) + hops(dq // across, wide) + hops(dq % across, across)
+
+    chip_offsets.sort(key=lambda offset: -distance(offset))
     tile_offsets = [2 * dq + dc for dq in chip_order for dc in (0, 1) if dq or dc]
 
     loads = {

time: 40.8 us -> 40.6 us (level)
  no operation moved by 1% of the time
where the time goes in v5:
time: 40.6 us; the launch traced here: 40.5 us
  Pallas kernels  39.8 us (98%)
  between operations  0.64 us (2%)
    pallas_call x1, Pallas kernels, body(): pl.pallas_call(functools.partial(kernel, groups, tiles), out_shape=(jax.S...  38.2 us
    pallas_call x1, Pallas kernels, body(): pl.pallas_call(finish, out_shape=(jax.ShapeDtypeStruct((lev, cols), F32),...  1.57 us

profile of v5, /device:TPU:1, one launch (start us, length us, event | category | flops | bytes accessed | tf_op | source)
XLA Modules:
  0.0 40.5 jit_solution(9098036329903392903)
XLA Ops:
  0.6 38.2 %shard_map.131 = (f32[128,4096]{1,0:T(8,128)S(1)}, f32[64,2560]{1,0:T(8,128)S(1)}, f32[1,4096]{1,0:T(1,128)S(1)}, f32[128,128]{1,0:T(8,128)S(1)}) custom-call(f32[128,4096]{1,0:T(8,128)} %state_hbm.1, f32[128,128]{1,0:T(8,128)} %vco_hbm.1, f32[1,128]{1,0:T(1,128)} %bitcast.9, bf16[8,128,128]{2,1,0:T(8,128)(2,1)} %blocks_hbm.1, s32[4,1280]{1,0:T(4,128)} %bitcast.6, ...), custom_call_target="tpu_custom_call" | custom-call | tf_op jit(solution)/shard_map/pallas_call | solution.py:619
  38.9 1.6 %shard_map.132 = (f32[128,4096]{1,0:T(8,128)}, f32[64,2560]{1,0:T(8,128)}) custom-call(f32[128,4096]{1,0:T(8,128)S(1)} %get-tuple-element.6.pre, f32[64,2560]{1,0:T(8,128)S(1)} %get-tuple-element.7.height, f32[1,4096]{1,0:T(1,128)S(1)} %get-tuple-element.8.rows, f32[128,128]{1,0:T(8,128)S(1)} %get-tuple-element.9.column), custom_call_target="tpu_custom_call" | custom-call | tf_op jit(solution)/shard_map/pallas_call | solution.py:699

commit v6 on v5

--- a/solution.py
+++ b/solution.py
@@ -157,7 +157,7 @@
 
     def load_state(i):
         part = pl.ds(i * chunk, chunk)
-        return pltpu.make_async_copy(state_hbm.at[:, part], state.at[:, part], in_sem.at[i])
+        return pltpu.make_async_copy(state_hbm.at[:, part], state.at[:, part], in_sem)
 
     barrier = pltpu.get_barrier_semaphore()
     greeted = [chip_peer(*d) for d in chip_offsets]
@@ -167,10 +167,11 @@
         for target in targets:
             pl.semaphore_signal(barrier, inc=1, device_id=target, device_id_type=MESH)
 
+    greet(greeted[:8])
     loads["vco"].start()
     for i in range(n_chunk):
         load_state(i).start()
-    greet(greeted)
+    greet(greeted[8:])
     loads["weight"].start()
     for name in loads:
         if name not in ("vco", "weight"):
@@ -191,8 +192,7 @@
         both = jnp.dot(vv[...], jnp.concatenate([hi, lo], axis=0), preferred_element_type=F32)
         return TIME_STEP * jnp.tanh(both[0:lev] + both[lev : 2 * lev])
 
-    for i in range(n_chunk):
-        load_state(i).wait()
+    pltpu.make_async_copy(state_hbm, state, in_sem).wait()
     loads["weight"].wait()
     column = jnp.transpose(jnp.broadcast_to(weight_ref[...], (LANES, lev)))[:, 0:1]
     parts = [pl.ds(i * chunk, chunk) for i in range(n_chunk)]
@@ -335,7 +335,7 @@
         return pltpu.make_async_remote_copy(
             src_ref=flux_all.at[slot],
             dst_ref=flux_all.at[slot],
-            send_sem=fwd_ssem.at[g],
+            send_sem=fwd_ssem,
             recv_sem=fwd_rsem.at[g],
             device_id=(group, partner),
             device_id_type=MESH,
@@ -575,8 +575,7 @@
 
     requests.wait_send()
     many(flux_all, (n_chip - 1) * nrows, flux_ssem, flux_rsem.at[0]).wait_send()
-    for g in range(groups):
-        forward(g).wait_send()
+    many(flux_all, half, fwd_ssem, flux_rsem.at[0]).wait_send()
     gram_all.wait_send()
     rows_all.wait_send()
 
@@ -658,12 +657,12 @@
                 pltpu.VMEM((n_req, LANES), BF16),
                 pltpu.VMEM((8, LANES), F32),
                 pltpu.VMEM((tiles * 8, LANES), F32),
-                dma((n_chunk,)),
+                dma,
                 dma((11,)),
                 dma((n_entry,)),
                 dma,
                 dma((groups,)),
-                dma((groups,)),
+                dma,
                 dma((groups,)),
                 dma,
                 dma,

time: 40.6 us -> 40.5 us (level)
  no operation moved by 1% of the time
where the time goes in v6:
time: 40.5 us; the launch traced here: 40.4 us
  Pallas kernels  39.8 us (98%)
  between operations  0.64 us (2%)
    pallas_call x1, Pallas kernels, body(): pl.pallas_call(functools.partial(kernel, groups, tiles), out_shape=(jax.S...  38.2 us
    pallas_call x1, Pallas kernels, body(): pl.pallas_call(finish, out_shape=(jax.ShapeDtypeStruct((lev, cols), F32),...  1.57 us

profile of v6, /device:TPU:1, one launch (start us, length us, event | category | flops | bytes accessed | tf_op | source)
XLA Modules:
  0.0 40.4 jit_solution(2637716230960661887)
XLA Ops:
  0.6 38.2 %shard_map.131 = (f32[128,4096]{1,0:T(8,128)S(1)}, f32[64,2560]{1,0:T(8,128)S(1)}, f32[1,4096]{1,0:T(1,128)S(1)}, f32[128,128]{1,0:T(8,128)S(1)}) custom-call(f32[128,4096]{1,0:T(8,128)} %state_hbm.1, f32[128,128]{1,0:T(8,128)} %vco_hbm.1, f32[1,128]{1,0:T(1,128)} %bitcast.9, bf16[8,128,128]{2,1,0:T(8,128)(2,1)} %blocks_hbm.1, s32[4,1280]{1,0:T(4,128)} %bitcast.6, ...), custom_call_target="tpu_custom_call" | custom-call | tf_op jit(solution)/shard_map/pallas_call | solution.py:618
  38.8 1.6 %shard_map.132 = (f32[128,4096]{1,0:T(8,128)}, f32[64,2560]{1,0:T(8,128)}) custom-call(f32[128,4096]{1,0:T(8,128)S(1)} %get-tuple-element.6.pre, f32[64,2560]{1,0:T(8,128)S(1)} %get-tuple-element.7.height, f32[1,4096]{1,0:T(1,128)S(1)} %get-tuple-element.8.rows, f32[128,128]{1,0:T(8,128)S(1)} %get-tuple-element.9.column), custom_call_target="tpu_custom_call" | custom-call | tf_op jit(solution)/shard_map/pallas_call | solution.py:698
